TPU v7x, 8 devices: a whole 2x2x1 slice. The times are simulated.
8 devices in a mesh: dp: 1 (over z), tp: 8 (over y, x, core).
Axes of the slice: x: 2, y: 2, z: 1, core: 2. Of those that a mesh axis runs over, the one named last changes fastest.
Arguments:
- hidden: bfloat16 [1, 512, 2560], P('dp')
- norm_w: bfloat16 [2, 2560], replicated
- w_z: bfloat16 [2, 2560, 5120], P(None, None, 'tp')
- w_x: bfloat16 [2, 2560, 5120], P(None, None, 'tp')
- w_bc: bfloat16 [2, 2560, 128], replicated
- w_dt: bfloat16 [2, 2560, 80], P(None, None, 'tp')
- conv_x: bfloat16 [2, 4, 5120], P(None, None, 'tp')
- conv_bc: bfloat16 [2, 4, 128], replicated
- bias_x: bfloat16 [2, 5120], P(None, 'tp')
- bias_bc: bfloat16 [2, 128], replicated
- dt_bias: float32 [2, 80], P(None, 'tp')
- a_log: float32 [2, 80], P(None, 'tp')
- d_skip: float32 [2, 80], P(None, 'tp')
- gate_w: bfloat16 [2, 5120], P(None, 'tp')
- w_out: bfloat16 [2, 5120, 2560], P(None, 'tp')
Outputs:
- output: bfloat16 [1, 512, 2560], P('dp')
All inputs are finite; a program needn't handle non-finite values.
Results may differ from a plain program's by a relative error of at most 0.0144688.
Values sent between devices are 32-bit elements.
A program may use at most 1 GiB of HBM per device.

v0:
```python
import jax
import jax.numpy as jnp
from jax import lax
from jax.sharding import PartitionSpec as P

EPSILON = 1e-5
CONV_WIDTH = 4
BLOCK_LEN = 256
FULL_PRECISION = lax.Precision.HIGHEST


def causal_conv(seq_in, kernel, conv_bias):
    n_steps = seq_in.shape[1]
    padded = jnp.pad(seq_in, ((0, 0), (CONV_WIDTH - 1, 0), (0, 0)))
    conv_sum = conv_bias.astype(jnp.float32)
    for tap_index in range(CONV_WIDTH):
        conv_sum = conv_sum + padded[:, tap_index:tap_index + n_steps, :].astype(jnp.float32) * kernel[tap_index].astype(jnp.float32)
    return conv_sum


def ssd_blocks(x_heads, dt_val, a_vals, b_in, c_in):
    n_batch, n_steps, n_heads, head_width = x_heads.shape
    n_state = b_in.shape[-1]
    n_blocks = n_steps // BLOCK_LEN
    x_blocks = x_heads.reshape(n_batch, n_blocks, BLOCK_LEN, n_heads, head_width)
    dt_blocks = dt_val.reshape(n_batch, n_blocks, BLOCK_LEN, n_heads)
    b_blocks = b_in.reshape(n_batch, n_blocks, BLOCK_LEN, n_state)
    c_blocks = c_in.reshape(n_batch, n_blocks, BLOCK_LEN, n_state)
    a_cum = jnp.cumsum(a_vals.reshape(n_batch, n_blocks, BLOCK_LEN, n_heads), axis=2)
    a_cum_t = jnp.swapaxes(a_cum, 2, 3)
    seg_sum = a_cum_t[..., :, None] - a_cum_t[..., None, :]
    step_ids = jnp.arange(BLOCK_LEN)
    lower_tri = step_ids[:, None] >= step_ids[None, :]
    c_dot_b = jnp.einsum('bcin,bcjn->bcij', c_blocks, b_blocks, precision=FULL_PRECISION)
    mix_mat = jnp.where(lower_tri, jnp.exp(jnp.minimum(seg_sum, 0.0)), 0.0) * c_dot_b[:, :, None]
    x_dt = x_blocks * dt_blocks[..., None]
    y_in = jnp.einsum('bchij,bcjhp->bcihp', mix_mat, x_dt, precision=FULL_PRECISION)
    a_last = a_cum[:, :, -1, :]
    tail_decay = jnp.exp(a_last[:, :, None, :] - a_cum)
    block_states = jnp.einsum('bcjn,bcjhp->bchpn', b_blocks, x_dt * tail_decay[..., None], precision=FULL_PRECISION)
    block_ends = jnp.swapaxes(jnp.cumsum(a_last, axis=1), 1, 2)
    block_starts = block_ends - jnp.swapaxes(a_last, 1, 2)
    block_ids = jnp.arange(n_blocks)
    earlier = block_ids[:, None] > block_ids[None, :]
    carry_mat = jnp.where(earlier, jnp.exp(jnp.minimum(block_starts[..., :, None] - block_ends[..., None, :], 0.0)), 0.0)
    s_in = jnp.einsum('bhck,bkhpn->bchpn', carry_mat, block_states, precision=FULL_PRECISION)
    y_st = jnp.einsum('bcin,bchpn->bcihp', c_blocks, s_in, precision=FULL_PRECISION) * jnp.exp(a_cum)[..., None]
    return (y_in + y_st).reshape(n_batch, n_steps, n_heads, head_width)


def mixer_layer(current, norm_w, w_z, w_x, w_bc, w_dt, conv_x, conv_bc, bias_x, bias_bc, dt_bias, a_log, d_skip, gate_w, w_out, inner_width):
    n_batch = current.shape[0]
    n_steps = current.shape[1]
    n_heads = dt_bias.shape[0]
    local_width = w_x.shape[-1]
    state_dim = w_bc.shape[-1] // 2
    residual = current.astype(jnp.float32)
    normed = (residual * lax.rsqrt(jnp.mean(residual * residual, axis=-1, keepdims=True) + EPSILON) * norm_w.astype(jnp.float32)).astype(jnp.bfloat16)
    gate_z = jnp.einsum('btd,de->bte', normed, w_z, preferred_element_type=jnp.float32).astype(jnp.bfloat16)
    x_pre = jnp.einsum('btd,de->bte', normed, w_x, preferred_element_type=jnp.float32).astype(jnp.bfloat16)
    bc_pre = jnp.einsum('btd,de->bte', normed, w_bc, preferred_element_type=jnp.float32).astype(jnp.bfloat16)
    dt_pre = jnp.einsum('btd,de->bte', normed, w_dt, preferred_element_type=jnp.float32).astype(jnp.bfloat16)
    x_act = jax.nn.silu(causal_conv(x_pre, conv_x, bias_x))
    bc_act = jax.nn.silu(causal_conv(bc_pre, conv_bc, bias_bc))
    dt_val = jax.nn.softplus(dt_pre.astype(jnp.float32) + dt_bias)
    a_vals = -dt_val * jnp.exp(a_log)
    x_heads = x_act.reshape(n_batch, n_steps, n_heads, local_width // n_heads)
    y_heads = ssd_blocks(x_heads, dt_val, a_vals, bc_act[..., :state_dim], bc_act[..., state_dim:]) + d_skip[:, None] * x_heads
    gated_v = y_heads.reshape(n_batch, n_steps, local_width) * jax.nn.silu(gate_z.astype(jnp.float32))
    part_sq = jnp.sum(gated_v * gated_v, axis=-1, keepdims=True)
    total_sq = lax.psum(part_sq, 'tp')
    normed_y = (gated_v * lax.rsqrt(total_sq / inner_width + EPSILON) * gate_w.astype(jnp.float32)).astype(jnp.bfloat16)
    part_out = jnp.einsum('bte,ed->btd', normed_y, w_out, preferred_element_type=jnp.float32)
    full_out = lax.psum(part_out, 'tp')
    return (residual + full_out).astype(jnp.bfloat16)


def solution(mesh):
    tp_size = mesh.shape['tp']
    rep_spec = P()
    col_spec = P(None, None, 'tp')
    vec_spec = P(None, 'tp')
    in_specs = (P('dp'), rep_spec, col_spec, col_spec, rep_spec, col_spec, col_spec, rep_spec, vec_spec, rep_spec, vec_spec, vec_spec, vec_spec, vec_spec, P(None, 'tp', None))

    def device_forward(hidden, norm_w, w_z, w_x, w_bc, w_dt, conv_x, conv_bc, bias_x, bias_bc, dt_bias, a_log, d_skip, gate_w, w_out):
        inner_width = w_x.shape[-1] * tp_size
        current = hidden
        for layer_idx in range(norm_w.shape[0]):
            current = mixer_layer(current, norm_w[layer_idx], w_z[layer_idx], w_x[layer_idx], w_bc[layer_idx], w_dt[layer_idx], conv_x[layer_idx], conv_bc[layer_idx], bias_x[layer_idx], bias_bc[layer_idx], dt_bias[layer_idx], a_log[layer_idx], d_skip[layer_idx], gate_w[layer_idx], w_out[layer_idx], inner_width)
        return current

    return jax.shard_map(device_forward, mesh=mesh, in_specs=in_specs, out_specs=P('dp'), check_vma=False)
```

profile of v0, /device:TPU:0, one launch (start us, length us, event | category | flops | bytes accessed | tf_op | source)
XLA Modules:
  0.0 348.1 jit_solution(4988368455967783308)
XLA Ops:
  6.7 2.5 fusion
  15.3 2.2 convolution_convert_fusion.1
  18.8 4.2 %fusion.62 = bf16[512,640]{1,0:T(8,128)(2,1)S(1)} fusion(bf16[2,2560,640]{2,1,0:T(8,128)(2,1)} %param.18, bf16[1,512,2560]{2,1,0:T(8,128)(2,1)S(1)} %copy-done, f32[2560]{0:T(1024)S(1)} %get-tuple-element.14, f32[512]{0:T(512)S(1)} %add_rsqrt_fusion.3), kind=kOutput, calls=%fused_computation.68 | convolution fusion | flops 1683292160 | bytes 6565888 | tf_op jit(solution)/shard_map/btd,de->bte/dot_general | solution.py:60
  22.9 2.0 divide_multiply_fusion.1
  24.9 2.8 copy.124
  27.7 3.4 reshape_reshape.6
  31.7 2.1 broadcast_multiply_fusion.2
  33.8 1.2 fusion.87
  35.1 2.6 convolution_bitcast_fusion.3
  38.9 5.9 %fusion.59 = f32[1,2,256,10,64]{2,4,3,1,0:T(8,128)S(1)} fusion(f32[1,2,256,10,64]{2,4,3,1,0:T(8,128)S(1)} %fusion.49, f32[2,256,256]{2,1,0:T(8,128)S(1)} %fusion.117, f32[2,10,256]{2,1,0:T(8,128)S(1)} %copy.130, pred[256,256]{1,0:T(8,128)(4,1)S(1)} %iota_compare_fusion, f32[2,256,10,64]{1,0,3,2:T(2,128)S(1)} %get-tuple-element.28), kind=kOutput, calls=%fused_computation.67 | convolution fusion | flops 1012203520 | bytes 4542464 | tf_op jit(solution)/shard_map/bchij,bcjhp->bcihp/dot_general | solution.py:37
  47.0 3.0 copy.149
  50.0 6.1 %multiply_reduce_fusion.1 = (f32[512]{0:T(512)S(1)}, f32[512,640]{1,0:T(8,128)}) fusion(bf16[2,2560,640]{2,1,0:T(8,128)(2,1)} %param.17, bf16[1,512,2560]{2,1,0:T(8,128)(2,1)S(1)} %copy-done, f32[2560]{0:T(1024)S(1)} %get-tuple-element.14, f32[512]{0:T(512)S(1)} %add_rsqrt_fusion.3, f32[512,640]{1,0:T(8,128)} %copy.149, ...), kind=kOutput, calls=%fused_computation.96 | convolution fusion | flops 1686568448 | bytes 9847296 | tf_op jit(solution)/shard_map/btd,de->bte/dot_general | solution.py:59
  56.1 25.0 %psum.28 = f32[1,512,1]{1,2,0:T(1,128)S(1)} all-reduce(f32[1,512,1]{1,2,0:T(1,128)S(1)} %bitcast.318), channel_id=1, replica_groups=mesh['dp'=1,'tp'=8] {'tp'}, use_global_device_ids=true, to_apply=%region_5.6 | all-reduce | flops 512 | bytes 4096 | tf_op jit(solution)/shard_map/psum | solution.py:71
  81.1 6.9 %convolution_bitcast_fusion.1 = f32[1,512,2560]{2,1,0:T(8,128)} fusion(bf16[2,640,2560]{2,1,0:T(8,128)(2,1)} %param.29, f32[512,640]{1,0:T(8,128)} %get-tuple-element.54, f32[640]{0:T(1024)S(1)} %get-tuple-element.16, f32[512]{0:T(512)S(1)} %bitcast.321), kind=kOutput, calls=%fused_computation.27 | convolution fusion | flops 1678704640 | bytes 9835008 | tf_op jit(solution)/shard_map/bte,ed->btd/dot_general | solution.py:73
  88.9 81.0 %all-reduce.7.cloned.1.call-done = f32[1,512,2560]{2,1,0:T(8,128)} async-done(((f32[1,512,2560]{2,1,0:T(8,128)}), f32[1,512,2560]{2,1,0:T(8,128)}) %all-reduce.7.cloned.1.call-update) | async-done | bytes 5242896 | tf_op jit(solution)/shard_map/psum | solution.py:74
  169.9 4.3 %fusion.4 = (f32[512]{0:T(512)S(1)}, bf16[1,512,2560]{2,1,0:T(8,128)(2,1)S(1)}) fusion(f32[1,512,2560]{2,1,0:T(8,128)} %all-reduce.7.cloned.1.call-done, bf16[1,512,2560]{2,1,0:T(8,128)(2,1)} %param.15), kind=kLoop, calls=%fused_computation.10 | loop fusion | flops 7863808 | bytes 10487808 | tf_op jit(solution)/shard_map/reduce_sum | solution.py:58
  174.2 1.5 negate_multiply_fusion
  177.4 2.2 convolution_convert_fusion
  179.6 4.2 %fusion.68 = bf16[512,640]{1,0:T(8,128)(2,1)S(1)} fusion(bf16[2,2560,640]{2,1,0:T(8,128)(2,1)} %param.18, bf16[1,512,2560]{2,1,0:T(8,128)(2,1)S(1)} %get-tuple-element.24, f32[2560]{0:T(1024)S(1)} %get-tuple-element.13, f32[512]{0:T(512)S(1)} %add_rsqrt_fusion.1), kind=kOutput, calls=%fused_computation.70 | convolution fusion | flops 1683292160 | bytes 6565888 | tf_op jit(solution)/shard_map/btd,de->bte/dot_general | solution.py:60
  186.3 1.4 mul.567
  190.4 2.7 divide_multiply_fusion
  193.1 2.8 copy.150
  195.9 3.2 reshape_reshape.7
  199.7 2.1 broadcast_multiply_fusion
  203.1 2.6 convolution_bitcast_fusion.2
  207.0 5.9 %fusion.56 = f32[1,2,256,10,64]{2,4,3,1,0:T(8,128)S(1)} fusion(f32[1,2,256,10,64]{2,4,3,1,0:T(8,128)S(1)} %fusion.48, f32[2,256,256]{2,1,0:T(8,128)S(1)} %fusion.114, f32[2,10,256]{2,1,0:T(8,128)S(1)} %copy-done.9, pred[256,256]{1,0:T(8,128)(4,1)S(1)} %copy-done.6, f32[2,256,10,64]{1,0,3,2:T(2,128)S(1)} %get-tuple-element.22), kind=kOutput, calls=%fused_computation.66 | convolution fusion | flops 1012203520 | bytes 4542464 | tf_op jit(solution)/shard_map/bchij,bcjhp->bcihp/dot_general | solution.py:37
  215.1 3.0 copy.175
  218.1 6.1 %multiply_reduce_fusion = (f32[512]{0:T(512)S(1)}, f32[512,640]{1,0:T(8,128)}) fusion(bf16[2,2560,640]{2,1,0:T(8,128)(2,1)} %param.17, bf16[1,512,2560]{2,1,0:T(8,128)(2,1)S(1)} %get-tuple-element.24, f32[2560]{0:T(1024)S(1)} %copy-done.11, f32[512]{0:T(512)S(1)} %copy-done.20, f32[512,640]{1,0:T(8,128)} %copy.175, f32[1,512,640]{2,1,0:T(8,128)} %divide_multiply_fusion, ...), kind=kOutput, calls=%fused_computation.93 | convolution fusion | flops 1686568448 | bytes 9847296 | tf_op jit(solution)/shard_map/btd,de->bte/dot_general | solution.py:59
  224.3 22.3 %psum.30 = f32[1,512,1]{1,2,0:T(1,128)S(1)} all-reduce(f32[1,512,1]{1,2,0:T(1,128)S(1)} %bitcast.319), channel_id=1, replica_groups=mesh['dp'=1,'tp'=8] {'tp'}, use_global_device_ids=true, to_apply=%region_12.13 | all-reduce | flops 512 | bytes 4096 | tf_op jit(solution)/shard_map/psum | solution.py:71
  246.6 6.9 %convolution_bitcast_fusion = f32[1,512,2560]{2,1,0:T(8,128)} fusion(bf16[2,640,2560]{2,1,0:T(8,128)(2,1)} %param.29, f32[512,640]{1,0:T(8,128)} %get-tuple-element.58, f32[640]{0:T(1024)S(1)} %copy-done.16, f32[512]{0:T(512)S(1)} %bitcast.320), kind=kOutput, calls=%fused_computation.26 | convolution fusion | flops 1678704640 | bytes 9835008 | tf_op jit(solution)/shard_map/bte,ed->btd/dot_general | solution.py:73
  253.5 82.6 %all-reduce.9.cloned.1.call-done = f32[1,512,2560]{2,1,0:T(8,128)} async-done(((f32[1,512,2560]{2,1,0:T(8,128)}), f32[1,512,2560]{2,1,0:T(8,128)}) %all-reduce.9.cloned.1.call-update) | async-done | bytes 5242896 | tf_op jit(solution)/shard_map/psum | solution.py:74
  336.1 4.7 %fusion.7 = bf16[1,512,2560]{2,1,0:T(8,128)(2,1)} fusion(f32[1,512,2560]{2,1,0:T(8,128)} %all-reduce.9.cloned.1.call-done, bf16[1,512,2560]{2,1,0:T(8,128)(2,1)S(1)} %get-tuple-element.24), kind=kLoop, calls=%fused_computation.13 | loop fusion | flops 3932160 | bytes 10485760 | tf_op jit(solution)/shard_map/convert_element_type | solution.py:75
  (144 shorter events, 24.2 us)
Async XLA Ops:
  6.5 163.3 %all-reduce.7.cloned.1.call-start = ((), (), s32[]{:S(2)}) async-start(), calls=%async_computation | async-start | bytes 10485760 | tf_op jit(solution)/shard_map/psum | solution.py:74
  6.5 28.5 %copy-start.17 = (pred[2,2]{1,0:T(4,128)(4,1)}, pred[2,2]{1,0:T(4,128)(4,1)S(1)}, u32[]{:S(2)}) copy-start(pred[2,2]{1,0:T(4,128)(4,1)S(1)} %iota_compare_fusion.1) | copy-start | bytes 16
  6.5 2.6 copy-start.7
  6.6 2.7 copy-start.1
  6.6 32.3 %copy-start.5 = (pred[256,256]{1,0:T(8,128)(4,1)}, pred[256,256]{1,0:T(8,128)(4,1)S(1)}, u32[]{:S(2)}) copy-start(pred[256,256]{1,0:T(8,128)(4,1)S(1)} %iota_compare_fusion) | copy-start | bytes 196612
  6.6 2.8 copy-start.23
  6.6 2.8 copy-start.24
  6.6 2.8 copy-start
  9.2 170.4 %copy-start.10 = (f32[2560]{0:T(1024)}, f32[2560]{0:T(1024)S(1)}, u32[]{:S(2)}) copy-start(f32[2560]{0:T(1024)S(1)} %get-tuple-element.13) | copy-start | bytes 30724
  9.4 2.7 copy-start.21
  9.4 3.3 copy-start.22
  9.5 3.3 copy-start.14
  9.5 4.0 %copy-start.12 = (bf16[2,640]{1,0:T(2,128)(2,1)S(1)}, bf16[2,640]{1,0:T(2,128)(2,1)}, u32[]{:S(2)}) copy-start(bf16[2,640]{1,0:T(2,128)(2,1)} %param.23) | copy-start | bytes 7684
  9.5 4.6 %copy-start.13 = (bf16[2,640]{1,0:T(2,128)(2,1)S(1)}, bf16[2,640]{1,0:T(2,128)(2,1)}, u32[]{:S(2)}) copy-start(bf16[2,640]{1,0:T(2,128)(2,1)} %param.28) | copy-start | bytes 7684
  9.5 5.2 %copy-start.8 = (bf16[2,4,640]{2,1,0:T(4,128)(2,1)S(1)}, bf16[2,4,640]{2,1,0:T(4,128)(2,1)}, u32[]{:S(2)}) copy-start(bf16[2,4,640]{2,1,0:T(4,128)(2,1)} %param.21) | copy-start | bytes 30724
  88.1 248.0 %all-reduce.9.cloned.1.call-start = ((), (), s32[]{:S(2)}) async-start(), calls=%async_computation.1 | async-start | bytes 10485760 | tf_op jit(solution)/shard_map/psum | solution.py:74
  174.2 5.4 %copy-start.19 = (f32[512]{0:T(512)}, f32[512]{0:T(512)S(1)}, u32[]{:S(2)}) copy-start(f32[512]{0:T(512)S(1)} %add_rsqrt_fusion.1) | copy-start | bytes 6148
  195.9 3.8 %copy-start.3 = (f32[2,256,10]{1,0,2:T(2,128)S(1)}, f32[2,256,10]{1,0,2:T(2,128)}, u32[]{:S(2)}) copy-start(f32[2,256,10]{1,0,2:T(2,128)} %exponential_bitcast_fusion.1) | copy-start | bytes 61444
  195.9 3.8 %copy-start.4 = (f32[2,256,10]{1,0,2:T(2,128)S(1)}, f32[2,256,10]{1,0,2:T(2,128)}, u32[]{:S(2)}) copy-start(f32[2,256,10]{1,0,2:T(2,128)} %mul.567) | copy-start | bytes 61444
  201.8 1.3 copy-start.18
  201.8 3.9 %copy-start.2 = (f32[2,256,10]{1,2,0:T(8,128)S(1)}, f32[2,256,10]{1,2,0:T(8,128)}, u32[]{:S(2)}) copy-start(f32[2,256,10]{1,2,0:T(8,128)} %copy.173) | copy-start | bytes 61444
  205.7 1.2 copy-start.6
  205.7 1.2 copy-start.9
  215.0 3.1 copy-start.11
  215.0 3.1 copy-start.15
  215.1 3.1 copy-start.20
  218.1 28.5 %copy-start.16 = (f32[640]{0:T(1024)S(1)}, f32[640]{0:T(1024)}, u32[]{:S(2)}) copy-start(f32[640]{0:T(1024)} %get-tuple-element.15) | copy-start | bytes 7684
Sparse Core Ops, SparseCore 0:
  88.2 81.6 all-reduce.6
  253.7 82.4 all-reduce.8
where the time goes:
time: 354 us; the launch traced here: 348 us
  waiting for transfers between devices  164 us (46%)
  matrix products  64.3 us (18%)
  blocking collectives  47.3 us (13%)
  local copies, waits for them, and re-layouts  30.2 us (9%)
  other arithmetic  28.1 us (8%)
  between operations  14.6 us (4%)
    psum x2, waiting for transfers between devices, mixer_layer(): full_out = lax.psum(part_out, 'tp')  164 us
    psum x2, blocking collectives, mixer_layer(): total_sq = lax.psum(part_sq, 'tp')  47.3 us
    dot_general x2, matrix products, mixer_layer(): jnp.einsum('bte,ed->btd', normed_y, w_out, preferred_element_type=jnp.flo...  13.9 us
    dot_general x2, matrix products, mixer_layer(): jnp.einsum('btd,de->bte', normed, w_z, preferred_element_type=jnp.float32)  12.3 us
    dot_general x2, matrix products, ssd_blocks(): jnp.einsum('bchij,bcjhp->bcihp', mix_mat, x_dt, precision=FULL_PRECISION)  11.8 us
    dot_general x2, matrix products, mixer_layer(): jnp.einsum('btd,de->bte', normed, w_x, preferred_element_type=jnp.float32)  8.35 us
  transfers between devices with their start and end apart: 2, of which 2 were waited for; matrix products, arithmetic and copies ran while one was open for 0% of the time, Pallas kernels for 0%

commit v1 on v0

v1 whole, which is shorter than its diff:
```python
import functools

import jax
import jax.numpy as jnp
from jax import lax
from jax.experimental import pallas as pl
from jax.experimental.pallas import tpu as pltpu
from jax.sharding import PartitionSpec as P

EPS = 1e-5
T = 128
HEAD = 64
STATE = 64
HI = lax.Precision.HIGHEST
F32 = jnp.float32
BF16 = jnp.bfloat16


def mixer_kernel(n_layers, n_chunks, inner_width,
                 hid_ref, norm_ref, wz_ref, wx_ref, wbc_ref, wdt_ref, convx_ref, convbc_ref, biasx_ref,
                 biasbc_ref, dtb_ref, alog_ref, dskip_ref, gate_ref, wout_ref,
                 out_ref,
                 w_in, w_o, wdt_s, hid_s, u_buf, p_buf, r0, r1a, r1b, r2a, r2b, h_buf, c_buf, zd_buf,
                 x_act, v_buf, s_buf, cs_buf, acum_s, acumt_s, dt_s, g_s, bt_s, stats,
                 norm_s, cw_s, cb_s, dtb_s, nega_s, dsk_s, gate_s,
                 w_sem, h_sem, o_sem, send_sem, recv_sem, st_send, st_recv):
    d_model = u_buf.shape[2]
    width = x_act.shape[1]
    n_pairs = width // (2 * HEAD)
    n_heads = dtb_ref.shape[1]
    conv_w = width + 2 * STATE
    n_items = n_layers * n_chunks

    me = lax.axis_index("tp")
    core = lax.rem(me, 2)
    xi = lax.rem(me // 2, 2)
    yi = me // 4

    def peer_id(dx, dy, dc):
        px = xi if dx == 0 else 1 - xi
        py = yi if dy == 0 else 1 - yi
        pc = core if dc == 0 else 1 - core
        return {"tp": py * 4 + px * 2 + pc}

    relations = [(dx, dy, dc) for dx in (0, 1) for dy in (0, 1) for dc in (0, 1)][1:]
    core_peer, x_peer, y_peer = peer_id(0, 0, 1), peer_id(1, 0, 0), peer_id(0, 1, 0)

    def weight_copies(l):
        return [
            pltpu.make_async_copy(wx_ref.at[l], w_in.at[l, :, pl.ds(0, width)], w_sem.at[l, 0]),
            pltpu.make_async_copy(wbc_ref.at[l], w_in.at[l, :, pl.ds(width, 2 * STATE)], w_sem.at[l, 1]),
            pltpu.make_async_copy(wz_ref.at[l], w_in.at[l, :, pl.ds(conv_w + 128, width)], w_sem.at[l, 2]),
            pltpu.make_async_copy(wdt_ref.at[l], wdt_s.at[l], w_sem.at[l, 3]),
        ]

    def out_weight_copy(l):
        return pltpu.make_async_copy(wout_ref.at[l], w_o.at[l], w_sem.at[l, 4])

    def hid_copy(c):
        rows = pl.ds(c * T, T)
        return pltpu.make_async_copy(hid_ref.at[0, rows, :], hid_s.at[rows, :], h_sem.at[c])

    def out_copy(c):
        rows = pl.ds(c * T, T)
        return pltpu.make_async_copy(hid_s.at[rows, :], out_ref.at[0, rows, :], o_sem.at[c])

    hid_copy(0).start()
    for cp in weight_copies(0):
        cp.start()
    out_weight_copy(0).start()
    for c in range(1, n_chunks):
        hid_copy(c).start()
    for l in range(1, n_layers):
        for cp in weight_copies(l):
            cp.start()
        out_weight_copy(l).start()

    barrier = pltpu.get_barrier_semaphore()
    for rel in relations:
        pl.semaphore_signal(barrier, inc=1, device_id=peer_id(*rel))

    lane = lax.broadcasted_iota(jnp.int32, (1, 128), 1)
    for l in range(n_layers):
        norm_s[l] = norm_ref[l:l + 1, :].astype(F32)
        cw_s[l, :, 0:width] = convx_ref[l].astype(F32)
        cw_s[l, :, width:conv_w] = convbc_ref[l].astype(F32)
        cb_s[l, :, 0:width] = biasx_ref[l:l + 1, :].astype(F32)
        cb_s[l, :, width:conv_w] = biasbc_ref[l:l + 1, :].astype(F32)
        gate_s[l] = gate_ref[l:l + 1, :].astype(F32)
        dtb_s[l] = jnp.zeros((1, 128), F32)
        nega_s[l] = jnp.zeros((1, 128), F32)
        dtb_s[l, :, 0:n_heads] = dtb_ref[l:l + 1, :]
        nega_s[l, :, 0:n_heads] = -jnp.exp(alog_ref[l:l + 1, :])
        for p in range(n_pairs):
            d0 = dskip_ref[l:l + 1, 2 * p:2 * p + 1]
            d1 = dskip_ref[l:l + 1, 2 * p + 1:2 * p + 2]
            dsk_s[l, :, 128 * p:128 * (p + 1)] = jnp.where(lane < HEAD, d0, d1)

    def rdma(kind, j):
        l, c = j // n_chunks, lax.rem(j, n_chunks)
        base = pl.multiple_of(c * T, T)
        mine = pl.multiple_of(core * (T // 2), T // 2)
        theirs = pl.multiple_of((1 - core) * (T // 2), T // 2)
        if kind == 0:
            src, dst, dev = p_buf.at[lax.rem(j, 2), pl.ds(theirs, T // 2), :], r0.at[j], core_peer
        elif kind == 1:
            src, dst, dev = r0.at[j, pl.ds(pl.multiple_of((1 - xi) * 16, 16), 16), :], r1a.at[j], x_peer
        elif kind == 2:
            src, dst, dev = r0.at[j, pl.ds(pl.multiple_of(32 + (1 - yi) * 16, 16), 16), :], r1b.at[j], y_peer
        elif kind == 3:
            src, dst, dev = r1a.at[j, pl.ds(pl.multiple_of((1 - yi) * 8, 8), 8), :], r2a.at[j], y_peer
        elif kind == 4:
            src, dst, dev = r1b.at[j, pl.ds(pl.multiple_of((1 - xi) * 8, 8), 8), :], r2b.at[j], x_peer
        else:
            if kind == 5:
                off, size, dev = base + mine + xi * 16 + yi * 8, 8, y_peer
            elif kind == 6:
                off, size, dev = base + mine + 32 + yi * 16 + xi * 8, 8, x_peer
            elif kind == 7:
                off, size, dev = base + mine + xi * 16, 16, x_peer
            elif kind == 8:
                off, size, dev = base + mine + 32 + yi * 16, 16, y_peer
            else:
                off, size, dev = base + mine, T // 2, core_peer
            src = u_buf.at[l + 1, pl.ds(pl.multiple_of(off, 8), size), :]
            dst = src
        return pltpu.make_async_remote_copy(
            src_ref=src, dst_ref=dst, send_sem=send_sem.at[j, kind], recv_sem=recv_sem.at[j, kind],
            device_id=dev, device_id_type=pl.DeviceIdType.MESH)

    def stat_copy(r, j):
        return pltpu.make_async_remote_copy(
            src_ref=stats.at[j, pl.ds(0, 1), :], dst_ref=stats.at[j, pl.ds(r + 1, 1), :],
            send_sem=st_send.at[j, r], recv_sem=st_recv.at[j, r],
            device_id=peer_id(*relations[r]), device_id_type=pl.DeviceIdType.MESH)

    def in_proj(j):
        l, c = j // n_chunks, lax.rem(j, n_chunks)
        base = pl.multiple_of(c * T, T)

        @pl.when(l == 0)
        def _():
            hid_copy(c).wait()

            @pl.loop(0, T // 16)
            def _(i):
                rows = pl.ds(pl.multiple_of(base + i * 16, 16), 16)
                u_buf[0, rows, :] = hid_s[rows, :].astype(F32)

        @pl.loop(0, T // 16)
        def _(i):
            u = u_buf[l, pl.ds(pl.multiple_of(base + i * 16, 16), 16), :]
            ms = jnp.mean(u * u, axis=-1, keepdims=True)
            h = u * lax.rsqrt(ms + EPS) * norm_s[l]
            h_buf[pl.ds(pl.multiple_of(i * 16, 16), 16), :] = h.astype(BF16)

        @pl.when(c == 0)
        def _():
            for cp in weight_copies(l):
                cp.wait()

            @pl.loop(0, d_model // 256)
            def _(i):
                rows = pl.ds(pl.multiple_of(i * 256, 256), 256)
                w_in[l, rows, conv_w:conv_w + 128] = jnp.zeros((256, 128), BF16)
                w_in[l, rows, conv_w:conv_w + n_heads] = wdt_s[l, rows, :]

            c_buf[0:8, :] = jnp.zeros((8, conv_w), F32)
            s_buf[...] = jnp.zeros_like(s_buf)

        @pl.when(c > 0)
        def _():
            c_buf[0:8, :] = c_buf[T:T + 8, :]

        h = h_buf[...]
        for n in range(0, conv_w, 256):
            r = jnp.dot(h, w_in[l, :, n:n + 256], preferred_element_type=F32)
            c_buf[8:8 + T, n:n + 256] = r.astype(BF16).astype(F32)
        for n in range(0, width + 128, 256):
            r = jnp.dot(h, w_in[l, :, conv_w + n:conv_w + n + 256], preferred_element_type=F32)
            zd_buf[:, n:n + 256] = r.astype(BF16).astype(F32)

    def scan_prep(j):
        l = j // n_chunks
        b_act = None
        for n in range(0, conv_w, 128):
            cols = slice(n, n + 128)
            acc = cb_s[l, :, cols] + c_buf[5:5 + T, cols] * cw_s[l, 0:1, cols]
            for k in range(1, 4):
                acc = acc + c_buf[5 + k:5 + k + T, cols] * cw_s[l, k:k + 1, cols]
            act = acc * jax.nn.sigmoid(acc)
            if n < width:
                x_act[:, cols] = act
            else:
                b_act = act
        bt = b_act.T
        c_mat = b_act[:, STATE:2 * STATE]
        bt_s[...] = bt[0:STATE, :]
        g_s[...] = jnp.dot(c_mat, bt[0:STATE, :], precision=HI, preferred_element_type=F32)
        cs_buf[...] = jnp.dot(c_mat, s_buf[...], precision=HI, preferred_element_type=F32)
        dt = jax.nn.softplus(zd_buf[:, 0:128] + dtb_s[l])
        a = dt * nega_s[l]
        row = lax.broadcasted_iota(jnp.int32, (T, T), 0)
        col = lax.broadcasted_iota(jnp.int32, (T, T), 1)
        tril = jnp.where(row >= col, 1.0, 0.0).astype(F32)
        acum = jnp.dot(tril, a, precision=HI, preferred_element_type=F32)
        dt_s[...] = dt
        acum_s[...] = acum
        acumt_s[...] = acum.T

    def scan_heads(j):
        l = j // n_chunks
        slot = lax.rem(j, 2)
        row = lax.broadcasted_iota(jnp.int32, (T, T), 0)
        col = lax.broadcasted_iota(jnp.int32, (T, T), 1)
        causal = row >= col
        low = col < HEAD
        low_row = lane < HEAD
        g = g_s[...]
        bt = bt_s[...]
        sq = jnp.zeros((T, 128), F32)
        for p in range(n_pairs):
            h0, h1 = 2 * p, 2 * p + 1
            cols = slice(128 * p, 128 * (p + 1))
            a0 = jnp.broadcast_to(acum_s[:, h0:h0 + 1], (T, T))
            a1 = jnp.broadcast_to(acum_s[:, h1:h1 + 1], (T, T))
            m0 = jnp.where(causal, jnp.exp(jnp.minimum(a0 - acumt_s[h0:h0 + 1, :], 0.0)), 0.0) * g
            m1 = jnp.where(causal, jnp.exp(jnp.minimum(a1 - acumt_s[h1:h1 + 1, :], 0.0)), 0.0) * g
            dt = jnp.where(low, dt_s[:, h0:h0 + 1], dt_s[:, h1:h1 + 1])
            x = x_act[:, cols]
            xd = x * dt
            both = jnp.concatenate([m0, m1], axis=1)
            split = jnp.concatenate([jnp.where(low, xd, 0.0), jnp.where(low, 0.0, xd)], axis=0)
            y = jnp.dot(both, split, precision=HI, preferred_element_type=F32)
            ap = jnp.where(low, a0, a1)
            last = jnp.where(low_row, acum_s[T - 1:T, h0:h0 + 1], acum_s[T - 1:T, h1:h1 + 1])
            y = y + cs_buf[:, cols] * jnp.exp(ap)
            xt = xd * jnp.exp(last - ap)
            s_buf[:, cols] = s_buf[:, cols] * jnp.exp(last) + jnp.dot(bt, xt, precision=HI, preferred_element_type=F32)
            y = y + dsk_s[l, :, cols] * x
            z = zd_buf[:, 128 + 128 * p:256 + 128 * p]
            v = y * (z * jax.nn.sigmoid(z))
            v_buf[slot, :, cols] = v
            sq = sq + v * v
        ones = jnp.ones((8, 128), F32)
        part = lax.dot_general(ones, sq, (((1,), (1,)), ((), ())), precision=HI, preferred_element_type=F32)
        stats[j, 0:1, :] = part[0:1, :]
        for r in range(len(relations)):
            stat_copy(r, j).start()

    def out_proj(j):
        l, c = j // n_chunks, lax.rem(j, n_chunks)
        slot = lax.rem(j, 2)

        @pl.when(c == 0)
        def _():
            out_weight_copy(l).wait()

        for r in range(len(relations)):
            stat_copy(r, j).wait()
        total = jnp.sum(stats[j], axis=0, keepdims=True)
        rs = lax.rsqrt(total * (1.0 / inner_width) + EPS)
        rs_t = jnp.broadcast_to(rs, (T, T)).T
        parts = []
        for p in range(n_pairs):
            cols = slice(128 * p, 128 * (p + 1))
            parts.append((v_buf[slot, :, cols] * rs_t * gate_s[l, :, cols]).astype(BF16))
        g = jnp.concatenate(parts, axis=1)
        for n in range(0, d_model, 256):
            p_buf[slot, :, n:n + 256] = jnp.dot(g, w_o[l, :, n:n + 256], preferred_element_type=F32)
        rdma(0, j).start()

    def ev1(j):
        slot = lax.rem(j, 2)
        mine = core * (T // 2)
        rdma(0, j).wait()

        def add(off):
            off = pl.multiple_of(off, 16)
            r0[j, pl.ds(off, 16), :] += p_buf[slot, pl.ds(pl.multiple_of(mine + off, 16), 16), :]

        add((1 - xi) * 16)
        rdma(1, j).start()
        add(32 + (1 - yi) * 16)
        rdma(2, j).start()
        add(xi * 16)
        add(32 + yi * 16)

    def ev2(j):
        rdma(1, j).wait()
        r1a[j] += r0[j, pl.ds(pl.multiple_of(xi * 16, 16), 16), :]
        rdma(3, j).start()
        rdma(2, j).wait()
        r1b[j] += r0[j, pl.ds(pl.multiple_of(32 + yi * 16, 16), 16), :]
        rdma(4, j).start()

    def ev3(j):
        l, c = j // n_chunks, lax.rem(j, n_chunks)
        base = c * T + core * (T // 2)
        rows_a = pl.ds(pl.multiple_of(base + xi * 16 + yi * 8, 8), 8)
        rows_b = pl.ds(pl.multiple_of(base + 32 + yi * 16 + xi * 8, 8), 8)
        rdma(3, j).wait()
        val = r2a[j] + r1a[j, pl.ds(pl.multiple_of(yi * 8, 8), 8), :]
        u_buf[l + 1, rows_a, :] = (u_buf[l, rows_a, :] + val).astype(BF16).astype(F32)
        rdma(5, j).start()
        rdma(4, j).wait()
        val = r2b[j] + r1b[j, pl.ds(pl.multiple_of(xi * 8, 8), 8), :]
        u_buf[l + 1, rows_b, :] = (u_buf[l, rows_b, :] + val).astype(BF16).astype(F32)
        rdma(6, j).start()

    def ev4(j):
        rdma(5, j).wait()
        rdma(7, j).start()
        rdma(6, j).wait()
        rdma(8, j).start()

    def ev5(j):
        rdma(7, j).wait()
        rdma(8, j).wait()
        rdma(9, j).start()

    def ev6(j):
        l, c = j // n_chunks, lax.rem(j, n_chunks)
        rdma(9, j).wait()

        @pl.when(l == n_layers - 1)
        def _():
            @pl.loop(0, T // 16)
            def _(i):
                rows = pl.ds(pl.multiple_of(c * T + i * 16, 16), 16)
                hid_s[rows, :] = u_buf[n_layers, rows, :].astype(BF16)

            out_copy(c).start()

    def guarded(stage, j):
        pl.when(jnp.logical_and(j >= 0, j < n_items))(lambda: stage(j))

    pl.semaphore_wait(barrier, len(relations))

    @pl.loop(0, n_items + 3)
    def _(j):
        guarded(in_proj, j)
        guarded(ev2, j - 2)
        guarded(ev4, j - 3)
        guarded(out_proj, j - 1)
        guarded(scan_prep, j)
        guarded(ev1, j - 1)
        guarded(scan_heads, j)
        guarded(ev3, j - 2)
        guarded(ev5, j - 3)
        guarded(ev6, j - 3)

    for c in range(n_chunks):
        out_copy(c).wait()


def solution(mesh):
    tp_size = mesh.shape['tp']
    rep_spec = P()
    col_spec = P(None, None, 'tp')
    vec_spec = P(None, 'tp')
    in_specs = (P('dp'), rep_spec, col_spec, col_spec, rep_spec, col_spec, col_spec, rep_spec, vec_spec, rep_spec,
                vec_spec, vec_spec, vec_spec, vec_spec, P(None, 'tp', None))

    def device_forward(hidden, norm_w, w_z, w_x, w_bc, w_dt, conv_x, conv_bc, bias_x, bias_bc, dt_bias, a_log,
                       d_skip, gate_w, w_out):
        n_layers, d_model = norm_w.shape
        n_tok = hidden.shape[1]
        width = w_x.shape[-1]
        n_heads = dt_bias.shape[-1]
        conv_w = width + 2 * STATE
        n_chunks = n_tok // T
        n_items = n_layers * n_chunks
        any_spec = pl.BlockSpec(memory_space=pl.ANY)
        vmem_spec = pl.BlockSpec(memory_space=pltpu.VMEM)
        dma = pltpu.SemaphoreType.DMA
        return pl.pallas_call(
            functools.partial(mixer_kernel, n_layers, n_chunks, width * tp_size),
            out_shape=jax.ShapeDtypeStruct(hidden.shape, BF16),
            in_specs=[any_spec, vmem_spec, any_spec, any_spec, any_spec, any_spec] + [vmem_spec] * 8 + [any_spec],
            out_specs=any_spec,
            scratch_shapes=[
                pltpu.VMEM((n_layers, d_model, conv_w + 128 + width), BF16),
                pltpu.VMEM((n_layers, width, d_model), BF16),
                pltpu.VMEM((n_layers, d_model, n_heads), BF16),
                pltpu.VMEM((n_tok, d_model), BF16),
                pltpu.VMEM((n_layers + 1, n_tok, d_model), F32),
                pltpu.VMEM((2, T, d_model), F32),
                pltpu.VMEM((n_items, T // 2, d_model), F32),
                pltpu.VMEM((n_items, T // 8, d_model), F32),
                pltpu.VMEM((n_items, T // 8, d_model), F32),
                pltpu.VMEM((n_items, T // 16, d_model), F32),
                pltpu.VMEM((n_items, T // 16, d_model), F32),
                pltpu.VMEM((T, d_model), BF16),
                pltpu.VMEM((T + 8, conv_w), F32),
                pltpu.VMEM((T, 128 + width), F32),
                pltpu.VMEM((T, width), F32),
                pltpu.VMEM((2, T, width), F32),
                pltpu.VMEM((STATE, width), F32),
                pltpu.VMEM((T, width), F32),
                pltpu.VMEM((T, 128), F32),
                pltpu.VMEM((128, T), F32),
                pltpu.VMEM((T, 128), F32),
                pltpu.VMEM((T, T), F32),
                pltpu.VMEM((STATE, T), F32),
                pltpu.VMEM((n_items, 8, T), F32),
                pltpu.VMEM((n_layers, 1, d_model), F32),
                pltpu.VMEM((n_layers, 4, conv_w), F32),
                pltpu.VMEM((n_layers, 1, conv_w), F32),
                pltpu.VMEM((n_layers, 1, 128), F32),
                pltpu.VMEM((n_layers, 1, 128), F32),
                pltpu.VMEM((n_layers, 1, width), F32),
                pltpu.VMEM((n_layers, 1, width), F32),
                dma((n_layers, 5)),
                dma((n_chunks,)),
                dma((n_chunks,)),
                dma((n_items, 10)),
                dma((n_items, 10)),
                dma((n_items, 7)),
                dma((n_items, 7)),
            ],
            compiler_params=pltpu.CompilerParams(
                collective_id=0, has_side_effects=True, vmem_limit_bytes=67043328),
            name="mixer",
        )(hidden, norm_w, w_z, w_x, w_bc, w_dt, conv_x, conv_bc, bias_x, bias_bc, dt_bias, a_log, d_skip, gate_w,
          w_out)

    return jax.shard_map(device_forward, mesh=mesh, in_specs=in_specs, out_specs=P('dp'), check_vma=False)
```

time: 354 us -> 130 us (0.37); the launches traced: 348 us -> 130 us
  waiting for transfers between devices: 164 us -> 0 us
  Pallas kernels: 0 us -> 124 us
  matrix products: 64.3 us -> 0 us
  blocking collectives: 47.3 us -> 0 us
  other arithmetic: 28.1 us -> 0 us
  local copies, waits for them, and re-layouts: 30.2 us -> 5.64 us
  between operations: 14.6 us -> 0.01 us
    psum x2 -> x0, waiting for transfers between devices: 164 us -> none  [mixer_layer(): full_out = lax.psum(part_out, 'tp')]
    pallas_call x0 -> x1, Pallas kernels: none -> 124 us  [device_forward(): pl.pallas_call(functools.partial(mixer_kernel, n_layers, n_chunks, width...]
    dot_general x20 -> x0, matrix products: 64.3 us -> none  [the longest x2 13.9 us: mixer_layer(): jnp.einsum('bte,ed->btd', normed_y, w_out, preferred_element_type=jnp.flo...]
    psum x2 -> x0, blocking collectives: 47.3 us -> none  [mixer_layer(): total_sq = lax.psum(part_sq, 'tp')]
    mul x12 -> x0, other arithmetic: 12.1 us -> none  [the longest x4 4.96 us: ssd_blocks(): x_dt * tail_decay[..., None]]
    another operation x26 -> x0, local copies, waits for them, and re-layouts: 9.2 us -> none  [the longest x2 6.57 us: ssd_blocks(): x_heads.reshape(n_batch, n_blocks, BLOCK_LEN, n_heads, head_width)]
    mul x11 -> x0, local copies, waits for them, and re-layouts: 8.46 us -> none  [the longest x2 5.58 us: mixer_layer(): x_act = jax.nn.silu(causal_conv(x_pre, conv_x, bias_x))]
    reduce_sum x2 -> x0, other arithmetic: 6.76 us -> none  [mixer_layer(): jnp.mean(residual * residual, axis=-1, keepdims=True) + EPSILON]
  transfers between devices with their start and end apart: 2 -> 0, of which waited for: 2 -> 0; matrix products, arithmetic and copies ran while one was open for 0% -> 0% of each run, Pallas kernels for 0% -> 0%
where the time goes in v1:
time: 130 us
  Pallas kernels  124 us (95%)
  local copies, waits for them, and re-layouts  5.64 us (4%)
    pallas_call x1, Pallas kernels, device_forward(): pl.pallas_call(functools.partial(mixer_kernel, n_layers, n_chunks, width...  124 us
    unnamed x2, local copies, waits for them, and re-layouts  5.64 us

profile of v1, /device:TPU:0, one launch (start us, length us, event | category | flops | bytes accessed | tf_op | source)
XLA Modules:
  0.0 129.9 jit_solution(17250557037536809594)
XLA Ops:
  0.0 2.2 %copy.16.wdt_ref = bf16[2,2560,10]{2,1,0:T(8,128)(2,1)} copy(bf16[2,2560,10]{1,0,2:T(2,128)(2,1)} %param.20) | data formatting | bytes 204800 | tf_op args[5]
  2.2 124.2 %mixer.1 = bf16[1,512,2560]{2,1,0:T(8,128)(2,1)} custom-call(bf16[1,512,2560]{2,1,0:T(8,128)(2,1)} %hid_ref.1, bf16[2,2560]{1,0:T(2,128)(2,1)} %norm_ref.1, bf16[2,2560,640]{2,1,0:T(8,128)(2,1)} %wz_ref.1, bf16[2,2560,640]{2,1,0:T(8,128)(2,1)} %wx_ref.1, bf16[2,2560,128]{2,1,0:T(8,128)(2,1)} %wbc_ref.1, bf16[2,2560,10]{2,1,0:T(8,128)(2,1)} %copy.16.wdt_ref, ...), custom_call_target="tpu_custom_call" | custom-call | tf_op jit(solution)/shard_map/mixer/pallas_call | solution.py:377
  126.5 3.4 %copy.18 = bf16[1,512,2560]{2,1,0:T(8,128)(2,1)} copy(bf16[1,512,2560]{2,1,0:T(8,128)(2,1)} %mixer.1) | data formatting | bytes 5242880

commit v2 on v1

v2 whole, which is shorter than its diff:
```python
import functools

import jax
import jax.numpy as jnp
from jax import lax
from jax.experimental import pallas as pl
from jax.experimental.pallas import tpu as pltpu
from jax.sharding import PartitionSpec as P

EPS = 1e-5
T = 128
HEAD = 64
STATE = 64
HI = lax.Precision.HIGHEST
F32 = jnp.float32
BF16 = jnp.bfloat16


def mixer_kernel(n_layers, n_chunks, inner_width,
                 hid_ref, norm_ref, wz_ref, wx_ref, wbc_ref, wdt_ref, convx_ref, convbc_ref, biasx_ref,
                 biasbc_ref, dtb_ref, alog_ref, dskip_ref, gate_ref, wout_ref,
                 out_ref,
                 w_in, w_o, wdt_s, wdt_f, hid_s, u_buf, p_buf, r0, r1a, r1b, r2a, r2b, h_buf, c_buf, zd_buf,
                 x_act, v_buf, g_buf, s_buf, cs_buf, acum_s, acumt_s, dt_s, g_s, bt_s, sq_s, f_s, stats,
                 norm_s, cw_s, cb_s, dtb_s, nega_s, dsk_s, gate_s,
                 w_sem, h_sem, o_sem, send_sem, recv_sem, st_send, st_recv):
    d_model = u_buf.shape[2]
    half = d_model // 2
    width = x_act.shape[1]
    n_pairs = width // (2 * HEAD)
    n_heads = dtb_ref.shape[1]
    conv_w = width + 2 * STATE
    n_items = n_layers * n_chunks

    me = lax.axis_index("tp")
    core = lax.rem(me, 2)
    xi = lax.rem(me // 2, 2)
    yi = me // 4

    def peer_id(dx, dy, dc):
        px = xi if dx == 0 else 1 - xi
        py = yi if dy == 0 else 1 - yi
        pc = core if dc == 0 else 1 - core
        return {"tp": py * 4 + px * 2 + pc}

    relations = [(dx, dy, dc) for dx in (0, 1) for dy in (0, 1) for dc in (0, 1)][1:]
    core_peer, x_peer, y_peer = peer_id(0, 0, 1), peer_id(1, 0, 0), peer_id(0, 1, 0)

    def split_item(j):
        if isinstance(j, int):
            return j // n_chunks, j % n_chunks
        return j // n_chunks, lax.rem(j, n_chunks)

    halves = [slice(0, half), slice(half, d_model)]

    def at(off, size, unit=8):
        return pl.ds(pl.multiple_of(off, unit), size)

    def conv_weight_copies(l):
        return [
            pltpu.make_async_copy(wx_ref.at[l], w_in.at[l, :, pl.ds(0, width)], w_sem.at[l, 0]),
            pltpu.make_async_copy(wbc_ref.at[l], w_in.at[l, :, pl.ds(width, 2 * STATE)], w_sem.at[l, 0]),
        ]

    def gate_weight_copy(l):
        return pltpu.make_async_copy(wz_ref.at[l], w_in.at[l, :, pl.ds(conv_w + 128, width)], w_sem.at[l, 1])

    def out_weight_copy(l):
        return pltpu.make_async_copy(wout_ref.at[l], w_o.at[l], w_sem.at[l, 2])

    def dt_weight_copy():
        return pltpu.make_async_copy(wdt_ref, wdt_s, h_sem.at[2])

    def hid_copy(k):
        rows = pl.ds(0, T) if k == 0 else pl.ds(T, (n_chunks - 1) * T)
        return pltpu.make_async_copy(hid_ref.at[0, rows, :], hid_s.at[rows, :], h_sem.at[k])

    def out_copy(c, h):
        rows, cols = at(c * T, T, T), pl.ds(h * half, half)
        return pltpu.make_async_copy(hid_s.at[rows, cols], out_ref.at[0, rows, cols], o_sem)

    def start_in_weights(l):
        for cp in conv_weight_copies(l):
            cp.start()
        gate_weight_copy(l).start()

    hid_copy(0).start()
    dt_weight_copy().start()
    start_in_weights(0)

    barrier = pltpu.get_barrier_semaphore()
    for rel in relations:
        pl.semaphore_signal(barrier, inc=1, device_id=peer_id(*rel))

    lane = lax.broadcasted_iota(jnp.int32, (1, 128), 1)
    for l in range(n_layers):
        norm_s[l] = norm_ref[l:l + 1, :].astype(F32)
        cw_s[l, :, 0:width] = convx_ref[l].astype(F32)
        cw_s[l, :, width:conv_w] = convbc_ref[l].astype(F32)
        cb_s[l, :, 0:width] = biasx_ref[l:l + 1, :].astype(F32)
        cb_s[l, :, width:conv_w] = biasbc_ref[l:l + 1, :].astype(F32)
        gate_s[l] = gate_ref[l:l + 1, :].astype(F32)
        dtb_s[l] = jnp.zeros((1, 128), F32)
        nega_s[l] = jnp.zeros((1, 128), F32)
        dtb_s[l, :, 0:n_heads] = dtb_ref[l:l + 1, :]
        nega_s[l, :, 0:n_heads] = -jnp.exp(alog_ref[l:l + 1, :])
        for p in range(n_pairs):
            d0 = dskip_ref[l:l + 1, 2 * p:2 * p + 1]
            d1 = dskip_ref[l:l + 1, 2 * p + 1:2 * p + 2]
            dsk_s[l, :, 128 * p:128 * (p + 1)] = jnp.where(lane < HEAD, d0, d1)

    def rdma(kind, j, h):
        l, c = split_item(j)
        cols = pl.ds(h * half, half)
        mine = core * (T // 2)
        base = c * T + mine
        group = (kind + 1) // 2
        if kind == 0:
            src, dst, dev = p_buf.at[at((1 - core) * (T // 2), T // 2), cols], r0.at[j, :, cols], core_peer
        elif kind == 1:
            src, dst, dev = r0.at[j, at((1 - xi) * 16, 16), cols], r1a.at[j, :, cols], x_peer
        elif kind == 2:
            src, dst, dev = r0.at[j, at(32 + (1 - yi) * 16, 16), cols], r1b.at[j, :, cols], y_peer
        elif kind == 3:
            src, dst, dev = r1a.at[j, at((1 - yi) * 8, 8), cols], r2a.at[j, :, cols], y_peer
        elif kind == 4:
            src, dst, dev = r1b.at[j, at((1 - xi) * 8, 8), cols], r2b.at[j, :, cols], x_peer
        else:
            off, size, dev = [
                (base + xi * 16 + yi * 8, 8, y_peer),
                (base + 32 + yi * 16 + xi * 8, 8, x_peer),
                (base + xi * 16, 16, x_peer),
                (base + 32 + yi * 16, 16, y_peer),
                (base, T // 2, core_peer),
            ][kind - 5]
            src = u_buf.at[l + 1, at(off, size), cols]
            dst = src
        return pltpu.make_async_remote_copy(
            src_ref=src, dst_ref=dst, send_sem=send_sem.at[c, h, group], recv_sem=recv_sem.at[c, h, group],
            device_id=dev, device_id_type=pl.DeviceIdType.MESH)

    def wait_pair(kind, j, h):
        _, c = split_item(j)
        group = (kind + 1) // 2
        size = 32 if kind in (1, 7) else 16
        both = r0.at[j, pl.ds(0, size), pl.ds(h * half, half)]
        pltpu.make_async_copy(both, both, send_sem.at[c, h, group]).wait()
        pltpu.make_async_copy(both, both, recv_sem.at[c, h, group]).wait()

    def stat_copy(r, j):
        _, c = split_item(j)
        return pltpu.make_async_remote_copy(
            src_ref=stats.at[j, pl.ds(0, 1), :], dst_ref=stats.at[j, pl.ds(r + 1, 1), :],
            send_sem=st_send.at[c], recv_sem=st_recv.at[c],
            device_id=peer_id(*relations[r]), device_id_type=pl.DeviceIdType.MESH)

    def wait_stats(j):
        _, c = split_item(j)
        rows = stats.at[j, pl.ds(1, len(relations)), :]
        pltpu.make_async_copy(rows, rows, st_send.at[c]).wait()
        pltpu.make_async_copy(rows, rows, st_recv.at[c]).wait()

    def in_norm(j):
        l, c = split_item(j)
        base = c * T

        @pl.when(j == 0)
        def _():
            hid_copy(0).wait()

        @pl.when(j == 1)
        def _():
            hid_copy(1).wait()
            for k in range(1, n_layers):
                start_in_weights(k)
                out_weight_copy(k).start()

        @pl.when(l == 0)
        def _():
            @pl.loop(0, T // 16)
            def _(i):
                rows = at(base + i * 16, 16, 16)
                u_buf[0, rows, :] = hid_s[rows, :].astype(F32)

        @pl.loop(0, T // 16)
        def _(i):
            u = u_buf[l, at(base + i * 16, 16, 16), :]
            ms = jnp.mean(u * u, axis=-1, keepdims=True)
            h = u * lax.rsqrt(ms + EPS) * norm_s[l]
            h_buf[at(i * 16, 16, 16), :] = h.astype(BF16)

        @pl.when(c == 0)
        def _():
            c_buf[0:8, :] = jnp.zeros((8, conv_w), F32)
            s_buf[...] = jnp.zeros_like(s_buf)

        @pl.when(c > 0)
        def _():
            c_buf[0:8, :] = c_buf[T:T + 8, :]

    def in_conv(j):
        l, c = split_item(j)

        @pl.when(j == 0)
        def _():
            dt_weight_copy().wait()
            for k in range(n_layers):
                wdt_f[16 * k + 8:16 * k + 16, :] = jnp.zeros((8, d_model), F32)
            for n in range(n_heads):
                rows = wdt_s[n].astype(F32)
                for k in range(n_layers):
                    wdt_f[16 * k + n:16 * k + n + 1, :] = rows[k:k + 1, :]

        @pl.when(c == 0)
        def _():
            w_in[l, :, conv_w:conv_w + 128] = jnp.zeros((d_model, 128), BF16)
            w_in[l, :, conv_w:conv_w + 16] = wdt_f[at(16 * l, 16), :].T.astype(BF16)
            both = w_in.at[l, :, pl.ds(0, conv_w)]
            pltpu.make_async_copy(both, both, w_sem.at[l, 0]).wait()

        h = h_buf[...]
        for n in range(0, conv_w, 256):
            r = jnp.dot(h, w_in[l, :, n:n + 256], preferred_element_type=F32)
            c_buf[8:8 + T, n:n + 256] = r.astype(BF16).astype(F32)

    def in_gate(j):
        l, c = split_item(j)

        @pl.when(c == 0)
        def _():
            gate_weight_copy(l).wait()

        @pl.when(j == 0)
        def _():
            out_weight_copy(0).start()
            hid_copy(1).start()

        h = h_buf[...]
        for n in range(0, width + 128, 256):
            r = jnp.dot(h, w_in[l, :, conv_w + n:conv_w + n + 256], preferred_element_type=F32)
            zd_buf[:, n:n + 256] = r.astype(BF16).astype(F32)

    def scan_prep(j):
        l, _ = split_item(j)
        b_act = None
        for n in range(0, conv_w, 128):
            cols = slice(n, n + 128)
            acc = cb_s[l, :, cols] + c_buf[5:5 + T, cols] * cw_s[l, 0:1, cols]
            for k in range(1, 4):
                acc = acc + c_buf[5 + k:5 + k + T, cols] * cw_s[l, k:k + 1, cols]
            act = acc * jax.nn.sigmoid(acc)
            if n < width:
                x_act[:, cols] = act
            else:
                b_act = act
        bt = b_act.T[0:STATE, :]
        c_mat = b_act[:, STATE:2 * STATE]
        bt_s[...] = bt
        g_s[...] = jnp.dot(c_mat, bt, precision=HI, preferred_element_type=F32)
        cs_buf[...] = jnp.dot(c_mat, s_buf[...], precision=HI, preferred_element_type=F32)
        dt = jax.nn.softplus(zd_buf[:, 0:128] + dtb_s[l])
        a = dt * nega_s[l]
        row = lax.broadcasted_iota(jnp.int32, (T, T), 0)
        col = lax.broadcasted_iota(jnp.int32, (T, T), 1)
        tril = jnp.where(row >= col, 1.0, 0.0).astype(F32)
        acum = jnp.dot(tril, a, precision=HI, preferred_element_type=F32)
        dt_s[...] = dt
        acum_s[...] = acum
        acumt_s[...] = acum.T

    def scan_pairs(j, pairs):
        l, _ = split_item(j)
        row = lax.broadcasted_iota(jnp.int32, (T, T), 0)
        col = lax.broadcasted_iota(jnp.int32, (T, T), 1)
        causal = row >= col
        low = col < HEAD
        low_row = lane < HEAD
        g = g_s[...]
        bt = bt_s[...]
        sq = jnp.zeros((T, 128), F32)
        for p in pairs:
            h0, h1 = 2 * p, 2 * p + 1
            cols = slice(128 * p, 128 * (p + 1))
            a0 = jnp.broadcast_to(acum_s[:, h0:h0 + 1], (T, T))
            a1 = jnp.broadcast_to(acum_s[:, h1:h1 + 1], (T, T))
            m0 = jnp.where(causal, jnp.exp(jnp.minimum(a0 - acumt_s[h0:h0 + 1, :], 0.0)), 0.0) * g
            m1 = jnp.where(causal, jnp.exp(jnp.minimum(a1 - acumt_s[h1:h1 + 1, :], 0.0)), 0.0) * g
            dt = jnp.where(low, dt_s[:, h0:h0 + 1], dt_s[:, h1:h1 + 1])
            x = x_act[:, cols]
            xd = x * dt
            both = jnp.concatenate([m0, m1], axis=1)
            split = jnp.concatenate([jnp.where(low, xd, 0.0), jnp.where(low, 0.0, xd)], axis=0)
            y = jnp.dot(both, split, precision=HI, preferred_element_type=F32)
            ap = jnp.where(low, a0, a1)
            last = jnp.where(low_row, acum_s[T - 1:T, h0:h0 + 1], acum_s[T - 1:T, h1:h1 + 1])
            y = y + cs_buf[:, cols] * jnp.exp(ap)
            xt = xd * jnp.exp(last - ap)
            s_buf[:, cols] = s_buf[:, cols] * jnp.exp(last) + jnp.dot(bt, xt, precision=HI, preferred_element_type=F32)
            y = y + dsk_s[l, :, cols] * x
            z = zd_buf[:, 128 + 128 * p:256 + 128 * p]
            v = y * (z * jax.nn.sigmoid(z))
            v_buf[:, cols] = v
            sq = sq + v * v
        return sq

    first_pairs = (n_pairs + 1) // 2

    def scan_a(j):
        sq_s[...] = scan_pairs(j, range(first_pairs))

    def scan_b(j):
        l, _ = split_item(j)
        sq = sq_s[...] + scan_pairs(j, range(first_pairs, n_pairs))
        ones = jnp.ones((8, 128), F32)
        part = lax.dot_general(ones, sq, (((1,), (1,)), ((), ())), precision=HI, preferred_element_type=F32)
        stats[j, 0:1, :] = part[0:1, :]
        for r in range(len(relations)):
            stat_copy(r, j).start()
        own = lax.rsqrt(jnp.sum(sq, axis=1, keepdims=True) * (1.0 / width) + EPS)
        for p in range(n_pairs):
            cols = slice(128 * p, 128 * (p + 1))
            g_buf[:, cols] = (v_buf[:, cols] * own * gate_s[l, :, cols]).astype(BF16)

    def out_proj(j, h):
        l, c = split_item(j)
        if h == 0:
            @pl.when(c == 0)
            def _():
                out_weight_copy(l).wait()

        g = g_buf[...]
        for n in range(h * half, (h + 1) * half, 256):
            p_buf[:, n:n + 256] = jnp.dot(g, w_o[l, :, n:n + 256], preferred_element_type=F32)
        rdma(0, j, h).start()

    def factors(j):
        wait_stats(j)
        st = stats[j]
        rs = lax.rsqrt(jnp.sum(st, axis=0, keepdims=True) * (1.0 / inner_width) + EPS)
        for k in range(2):
            own = lax.rsqrt(st[k:k + 1, :] * (1.0 / width) + EPS)
            f = rs / jnp.maximum(own, 1e-30)
            f_s[k] = jnp.broadcast_to(f, (T, T)).T

    def ev1(j, h):
        if h == 1:
            factors(j)
        mine = core * (T // 2)
        rdma(0, j, h).wait()

        def add(off):
            f_me = f_s[0, at(mine + off, 16), :]
            f_peer = f_s[1, at(mine + off, 16), :]
            for n in range(h * half, (h + 1) * half, 128):
                cols = slice(n, n + 128)
                r0[j, at(off, 16), cols] = r0[j, at(off, 16), cols] * f_peer + p_buf[at(mine + off, 16), cols] * f_me

        add((1 - xi) * 16)
        rdma(1, j, h).start()
        add(32 + (1 - yi) * 16)
        rdma(2, j, h).start()
        add(xi * 16)
        add(32 + yi * 16)

    def ev2(j, h):
        cols = halves[h]
        wait_pair(1, j, h)
        r1a[j, :, cols] += r0[j, at(xi * 16, 16), cols]
        rdma(3, j, h).start()
        r1b[j, :, cols] += r0[j, at(32 + yi * 16, 16), cols]
        rdma(4, j, h).start()

    def ev3(j, h):
        l, c = split_item(j)
        cols = halves[h]
        base = c * T + core * (T // 2)
        rows_a = at(base + xi * 16 + yi * 8, 8)
        rows_b = at(base + 32 + yi * 16 + xi * 8, 8)
        wait_pair(3, j, h)
        val = r2a[j, :, cols] + r1a[j, at(yi * 8, 8), cols]
        u_buf[l + 1, rows_a, cols] = (u_buf[l, rows_a, cols] + val).astype(BF16).astype(F32)
        rdma(5, j, h).start()
        val = r2b[j, :, cols] + r1b[j, at(xi * 8, 8), cols]
        u_buf[l + 1, rows_b, cols] = (u_buf[l, rows_b, cols] + val).astype(BF16).astype(F32)
        rdma(6, j, h).start()

    def ev4(j, h):
        wait_pair(5, j, h)
        rdma(7, j, h).start()
        rdma(8, j, h).start()

    def ev5(j, h):
        wait_pair(7, j, h)
        rdma(9, j, h).start()

    def ev6(j, h):
        l, c = split_item(j)
        rdma(9, j, h).wait()

        def finish():
            @pl.loop(0, T // 16)
            def _(i):
                rows = at(c * T + i * 16, 16, 16)
                hid_s[rows, halves[h]] = u_buf[n_layers, rows, halves[h]].astype(BF16)

            out_copy(c, h).start()

        if isinstance(j, int):
            if l == n_layers - 1:
                finish()
        else:
            pl.when(l == n_layers - 1)(finish)

    def guarded(stage, j, *args):
        def run():
            with jax.named_scope(stage.__name__ + "".join(str(a) for a in args)):
                stage(j, *args)

        if isinstance(j, int):
            if 0 <= j < n_items:
                run()
        else:
            pl.when(jnp.logical_and(j >= 0, j < n_items))(run)

    pl.semaphore_wait(barrier, len(relations))

    @pl.loop(0, n_items)
    def _(j):
        guarded(ev6, j - 4, 0)
        guarded(in_norm, j)
        guarded(ev3, j - 2, 1)
        guarded(ev1, j - 1, 1)
        guarded(ev3, j - 2, 0)
        guarded(in_conv, j)
        guarded(ev5, j - 3, 1)
        guarded(ev1, j - 1, 0)
        guarded(in_gate, j)
        guarded(ev4, j - 2, 1)
        guarded(scan_prep, j)
        guarded(ev5, j - 3, 0)
        guarded(scan_a, j)
        guarded(ev2, j - 1, 1)
        guarded(scan_b, j)
        guarded(out_proj, j, 0)
        guarded(ev6, j - 3, 1)
        guarded(ev4, j - 2, 0)
        guarded(out_proj, j, 1)
        guarded(ev2, j - 1, 0)

    z = n_items - 1
    for stage, back, h in (
            (ev6, 3, 0), (ev5, 2, 1), (ev3, 1, 1), (ev6, 2, 1), (ev1, 0, 1), (ev1, 0, 0), (ev5, 2, 0), (ev3, 1, 0),
            (ev6, 2, 0), (ev4, 1, 1), (ev2, 0, 1), (ev2, 0, 0), (ev4, 1, 0), (ev5, 1, 1), (ev3, 0, 1), (ev6, 1, 1),
            (ev3, 0, 0), (ev5, 1, 0), (ev4, 0, 1), (ev6, 1, 0), (ev4, 0, 0), (ev5, 0, 1), (ev6, 0, 1), (ev5, 0, 0),
            (ev6, 0, 0)):
        guarded(stage, z - back, h)

    pltpu.make_async_copy(hid_s, out_ref.at[0], o_sem).wait()


def solution(mesh):
    tp_size = mesh.shape['tp']
    rep_spec = P()
    col_spec = P(None, None, 'tp')
    vec_spec = P(None, 'tp')
    in_specs = (P('dp'), rep_spec, col_spec, col_spec, rep_spec, col_spec, col_spec, rep_spec, vec_spec, rep_spec,
                vec_spec, vec_spec, vec_spec, vec_spec, P(None, 'tp', None))

    def device_forward(hidden, norm_w, w_z, w_x, w_bc, w_dt, conv_x, conv_bc, bias_x, bias_bc, dt_bias, a_log,
                       d_skip, gate_w, w_out):
        n_layers, d_model = norm_w.shape
        n_tok = hidden.shape[1]
        width = w_x.shape[-1]
        n_heads = dt_bias.shape[-1]
        conv_w = width + 2 * STATE
        n_chunks = n_tok // T
        n_items = n_layers * n_chunks
        any_spec = pl.BlockSpec(memory_space=pl.ANY)
        vmem_spec = pl.BlockSpec(memory_space=pltpu.VMEM)
        dma = pltpu.SemaphoreType.DMA
        return pl.pallas_call(
            functools.partial(mixer_kernel, n_layers, n_chunks, width * tp_size),
            out_shape=jax.ShapeDtypeStruct(hidden.shape, BF16),
            in_specs=[any_spec, vmem_spec, any_spec, any_spec, any_spec, any_spec] + [vmem_spec] * 8 + [any_spec],
            out_specs=any_spec,
            scratch_shapes=[
                pltpu.VMEM((n_layers, d_model, conv_w + 128 + width), BF16),
                pltpu.VMEM((n_layers, width, d_model), BF16),
                pltpu.VMEM((n_heads, n_layers, d_model), BF16),
                pltpu.VMEM((16 * n_layers, d_model), F32),
                pltpu.VMEM((n_tok, d_model), BF16),
                pltpu.VMEM((n_layers + 1, n_tok, d_model), F32),
                pltpu.VMEM((T, d_model), F32),
                pltpu.VMEM((n_items, T // 2, d_model), F32),
                pltpu.VMEM((n_items, 16, d_model), F32),
                pltpu.VMEM((n_items, 16, d_model), F32),
                pltpu.VMEM((n_items, 8, d_model), F32),
                pltpu.VMEM((n_items, 8, d_model), F32),
                pltpu.VMEM((T, d_model), BF16),
                pltpu.VMEM((T + 8, conv_w), F32),
                pltpu.VMEM((T, 128 + width), F32),
                pltpu.VMEM((T, width), F32),
                pltpu.VMEM((T, width), F32),
                pltpu.VMEM((T, width), BF16),
                pltpu.VMEM((STATE, width), F32),
                pltpu.VMEM((T, width), F32),
                pltpu.VMEM((T, 128), F32),
                pltpu.VMEM((128, T), F32),
                pltpu.VMEM((T, 128), F32),
                pltpu.VMEM((T, T), F32),
                pltpu.VMEM((STATE, T), F32),
                pltpu.VMEM((T, 128), F32),
                pltpu.VMEM((2, T, T), F32),
                pltpu.VMEM((n_items, 8, T), F32),
                pltpu.VMEM((n_layers, 1, d_model), F32),
                pltpu.VMEM((n_layers, 4, conv_w), F32),
                pltpu.VMEM((n_layers, 1, conv_w), F32),
                pltpu.VMEM((n_layers, 1, 128), F32),
                pltpu.VMEM((n_layers, 1, 128), F32),
                pltpu.VMEM((n_layers, 1, width), F32),
                pltpu.VMEM((n_layers, 1, width), F32),
                dma((n_layers, 3)),
                dma((3,)),
                dma(()),
                dma((n_chunks, 2, 6)),
                dma((n_chunks, 2, 6)),
                dma((n_chunks,)),
                dma((n_chunks,)),
            ],
            compiler_params=pltpu.CompilerParams(
                collective_id=0, has_side_effects=True, vmem_limit_bytes=67043328),
            name="mixer",
        )(hidden, norm_w, w_z, w_x, w_bc, jnp.transpose(w_dt, (2, 0, 1)), conv_x, conv_bc, bias_x, bias_bc, dt_bias,
          a_log, d_skip, gate_w, w_out)

    return jax.shard_map(device_forward, mesh=mesh, in_specs=in_specs, out_specs=P('dp'), check_vma=False)
```

time: 130 us -> 112 us (0.86)
  Pallas kernels: 124 us -> 108 us
  local copies, waits for them, and re-layouts: 5.64 us -> 3.4 us
    pallas_call x1, Pallas kernels: 124 us -> 108 us  [device_forward(): pl.pallas_call(functools.partial(mixer_kernel, n_layers, n_chunks, width...]
    unnamed x2 -> x1, local copies, waits for them, and re-layouts: 5.64 us -> 3.4 us
where the time goes in v2:
time: 112 us
  Pallas kernels  108 us (96%)
  local copies, waits for them, and re-layouts  3.4 us (3%)
    pallas_call x1, Pallas kernels, device_forward(): pl.pallas_call(functools.partial(mixer_kernel, n_layers, n_chunks, width...  108 us
    unnamed x1, local copies, waits for them, and re-layouts  3.4 us

profile of v2, /device:TPU:0, one launch (start us, length us, event | category | flops | bytes accessed | tf_op | source)
XLA Modules:
  0.0 111.7 jit_solution(9675368996450140601)
XLA Ops:
  0.0 108.3 %mixer.1 = bf16[1,512,2560]{2,1,0:T(8,128)(2,1)} custom-call(bf16[1,512,2560]{2,1,0:T(8,128)(2,1)} %hid_ref.1, bf16[2,2560]{1,0:T(2,128)(2,1)} %norm_ref.1, bf16[2,2560,640]{2,1,0:T(8,128)(2,1)} %wz_ref.1, bf16[2,2560,640]{2,1,0:T(8,128)(2,1)} %wx_ref.1, bf16[2,2560,128]{2,1,0:T(8,128)(2,1)} %wbc_ref.1, bf16[10,2,2560]{2,1,0:T(2,128)(2,1)} %bitcast.1, ...), custom_call_target="tpu_custom_call" | custom-call | tf_op jit(solution)/shard_map/mixer/pallas_call | solution.py:481
  108.3 3.4 %copy.17 = bf16[1,512,2560]{2,1,0:T(8,128)(2,1)} copy(bf16[1,512,2560]{2,1,0:T(8,128)(2,1)} %mixer.1) | data formatting | bytes 5242880

commit v3 on v2

--- a/solution.py
+++ b/solution.py
@@ -17,13 +17,14 @@
 
 
 def mixer_kernel(n_layers, n_chunks, inner_width,
-                 hid_ref, norm_ref, wz_ref, wx_ref, wbc_ref, wdt_ref, convx_ref, convbc_ref, biasx_ref,
-                 biasbc_ref, dtb_ref, alog_ref, dskip_ref, gate_ref, wout_ref,
+                 hid_ref, norm_hbm, wz_ref, wx_ref, wbc_ref, wdt_ref, convx_hbm, convbc_hbm, biasx_hbm,
+                 biasbc_hbm, dtb_hbm, alog_hbm, dskip_hbm, gate_hbm, wout_ref,
                  out_ref,
+                 norm_ref, convx_ref, convbc_ref, biasx_ref, biasbc_ref, dtb_ref, alog_ref, dskip_ref, gate_ref,
                  w_in, w_o, wdt_s, wdt_f, hid_s, u_buf, p_buf, r0, r1a, r1b, r2a, r2b, h_buf, c_buf, zd_buf,
                  x_act, v_buf, g_buf, s_buf, cs_buf, acum_s, acumt_s, dt_s, g_s, bt_s, sq_s, f_s, stats,
                  norm_s, cw_s, cb_s, dtb_s, nega_s, dsk_s, gate_s,
-                 w_sem, h_sem, o_sem, send_sem, recv_sem, st_send, st_recv):
+                 w_sem, h_sem, par_sem, send_sem, recv_sem, st_send, st_recv):
     d_model = u_buf.shape[2]
     half = d_model // 2
     width = x_act.shape[1]
@@ -51,6 +52,9 @@
             return j // n_chunks, j % n_chunks
         return j // n_chunks, lax.rem(j, n_chunks)
 
+    def slot_of(l):
+        return l % 2 if isinstance(l, int) else lax.rem(l, 2)
+
     halves = [slice(0, half), slice(half, d_model)]
 
     def at(off, size, unit=8):
@@ -75,16 +79,19 @@
         rows = pl.ds(0, T) if k == 0 else pl.ds(T, (n_chunks - 1) * T)
         return pltpu.make_async_copy(hid_ref.at[0, rows, :], hid_s.at[rows, :], h_sem.at[k])
 
-    def out_copy(c, h):
-        rows, cols = at(c * T, T, T), pl.ds(h * half, half)
-        return pltpu.make_async_copy(hid_s.at[rows, cols], out_ref.at[0, rows, cols], o_sem)
-
     def start_in_weights(l):
         for cp in conv_weight_copies(l):
             cp.start()
         gate_weight_copy(l).start()
 
+    small = [pltpu.make_async_copy(src, dst, par_sem.at[i]) for i, (src, dst) in enumerate((
+        (norm_hbm, norm_ref), (convx_hbm, convx_ref), (convbc_hbm, convbc_ref), (biasx_hbm, biasx_ref),
+        (biasbc_hbm, biasbc_ref), (dtb_hbm, dtb_ref), (alog_hbm, alog_ref), (dskip_hbm, dskip_ref),
+        (gate_hbm, gate_ref)))]
+
     hid_copy(0).start()
+    for cp in small:
+        cp.start()
     dt_weight_copy().start()
     start_in_weights(0)
 
@@ -92,6 +99,8 @@
     for rel in relations:
         pl.semaphore_signal(barrier, inc=1, device_id=peer_id(*rel))
 
+    for cp in small:
+        cp.wait()
     lane = lax.broadcasted_iota(jnp.int32, (1, 128), 1)
     for l in range(n_layers):
         norm_s[l] = norm_ref[l:l + 1, :].astype(F32)
@@ -116,15 +125,15 @@
         base = c * T + mine
         group = (kind + 1) // 2
         if kind == 0:
-            src, dst, dev = p_buf.at[at((1 - core) * (T // 2), T // 2), cols], r0.at[j, :, cols], core_peer
+            src, dst, dev = p_buf.at[at((1 - core) * (T // 2), T // 2), cols], r0.at[c, :, cols], core_peer
         elif kind == 1:
-            src, dst, dev = r0.at[j, at((1 - xi) * 16, 16), cols], r1a.at[j, :, cols], x_peer
+            src, dst, dev = r0.at[c, at((1 - xi) * 16, 16), cols], r1a.at[c, :, cols], x_peer
         elif kind == 2:
-            src, dst, dev = r0.at[j, at(32 + (1 - yi) * 16, 16), cols], r1b.at[j, :, cols], y_peer
+            src, dst, dev = r0.at[c, at(32 + (1 - yi) * 16, 16), cols], r1b.at[c, :, cols], y_peer
         elif kind == 3:
-            src, dst, dev = r1a.at[j, at((1 - yi) * 8, 8), cols], r2a.at[j, :, cols], y_peer
+            src, dst, dev = r1a.at[c, at((1 - yi) * 8, 8), cols], r2a.at[c, :, cols], y_peer
         elif kind == 4:
-            src, dst, dev = r1b.at[j, at((1 - xi) * 8, 8), cols], r2b.at[j, :, cols], x_peer
+            src, dst, dev = r1b.at[c, at((1 - xi) * 8, 8), cols], r2b.at[c, :, cols], x_peer
         else:
             off, size, dev = [
                 (base + xi * 16 + yi * 8, 8, y_peer),
@@ -133,7 +142,7 @@
                 (base + 32 + yi * 16, 16, y_peer),
                 (base, T // 2, core_peer),
             ][kind - 5]
-            src = u_buf.at[l + 1, at(off, size), cols]
+            src = u_buf.at[slot_of(l + 1), at(off, size), cols]
             dst = src
         return pltpu.make_async_remote_copy(
             src_ref=src, dst_ref=dst, send_sem=send_sem.at[c, h, group], recv_sem=recv_sem.at[c, h, group],
@@ -143,7 +152,7 @@
         _, c = split_item(j)
         group = (kind + 1) // 2
         size = 32 if kind in (1, 7) else 16
-        both = r0.at[j, pl.ds(0, size), pl.ds(h * half, half)]
+        both = r0.at[c, pl.ds(0, size), pl.ds(h * half, half)]
         pltpu.make_async_copy(both, both, send_sem.at[c, h, group]).wait()
         pltpu.make_async_copy(both, both, recv_sem.at[c, h, group]).wait()
 
@@ -175,19 +184,35 @@
                 start_in_weights(k)
                 out_weight_copy(k).start()
 
-        @pl.when(l == 0)
-        def _():
+        def squares(load):
             @pl.loop(0, T // 16)
             def _(i):
-                rows = at(base + i * 16, 16, 16)
-                u_buf[0, rows, :] = hid_s[rows, :].astype(F32)
+                acc = jnp.zeros((16, 128), F32)
+                for n in range(0, d_model, 128):
+                    u = load(base + i * 16, slice(n, n + 128))
+                    acc = acc + u * u
+                sq_s[at(i * 16, 16, 16), :] = acc
+
+        def load_hidden(off, cols):
+            u = hid_s[at(off, 16, 16), cols].astype(F32)
+            u_buf[0, at(off, 16, 16), cols] = u
+            return u
+
+        def load_u(off, cols):
+            return u_buf[slot_of(l), at(off, 16, 16), cols]
+
+        pl.when(l == 0)(lambda: squares(load_hidden))
+        pl.when(l > 0)(lambda: squares(load_u))
+        ms = jnp.sum(sq_s[...], axis=-1, keepdims=True) * (1.0 / d_model)
+        sq_s[...] = jnp.broadcast_to(lax.rsqrt(ms + EPS), (T, 128))
 
         @pl.loop(0, T // 16)
         def _(i):
-            u = u_buf[l, at(base + i * 16, 16, 16), :]
-            ms = jnp.mean(u * u, axis=-1, keepdims=True)
-            h = u * lax.rsqrt(ms + EPS) * norm_s[l]
-            h_buf[at(i * 16, 16, 16), :] = h.astype(BF16)
+            rs = sq_s[at(i * 16, 16, 16), :]
+            for n in range(0, d_model, 128):
+                cols = slice(n, n + 128)
+                h = load_u(base + i * 16, cols) * rs * norm_s[l, :, cols]
+                h_buf[at(i * 16, 16, 16), cols] = h.astype(BF16)
 
         @pl.when(c == 0)
         def _():
@@ -343,6 +368,7 @@
             f_s[k] = jnp.broadcast_to(f, (T, T)).T
 
     def ev1(j, h):
+        _, c = split_item(j)
         if h == 1:
             factors(j)
         mine = core * (T // 2)
@@ -353,7 +379,7 @@
             f_peer = f_s[1, at(mine + off, 16), :]
             for n in range(h * half, (h + 1) * half, 128):
                 cols = slice(n, n + 128)
-                r0[j, at(off, 16), cols] = r0[j, at(off, 16), cols] * f_peer + p_buf[at(mine + off, 16), cols] * f_me
+                r0[c, at(off, 16), cols] = r0[c, at(off, 16), cols] * f_peer + p_buf[at(mine + off, 16), cols] * f_me
 
         add((1 - xi) * 16)
         rdma(1, j, h).start()
@@ -363,11 +389,12 @@
         add(32 + yi * 16)
 
     def ev2(j, h):
+        _, c = split_item(j)
         cols = halves[h]
         wait_pair(1, j, h)
-        r1a[j, :, cols] += r0[j, at(xi * 16, 16), cols]
+        r1a[c, :, cols] += r0[c, at(xi * 16, 16), cols]
         rdma(3, j, h).start()
-        r1b[j, :, cols] += r0[j, at(32 + yi * 16, 16), cols]
+        r1b[c, :, cols] += r0[c, at(32 + yi * 16, 16), cols]
         rdma(4, j, h).start()
 
     def ev3(j, h):
@@ -377,11 +404,11 @@
         rows_a = at(base + xi * 16 + yi * 8, 8)
         rows_b = at(base + 32 + yi * 16 + xi * 8, 8)
         wait_pair(3, j, h)
-        val = r2a[j, :, cols] + r1a[j, at(yi * 8, 8), cols]
-        u_buf[l + 1, rows_a, cols] = (u_buf[l, rows_a, cols] + val).astype(BF16).astype(F32)
+        val = r2a[c, :, cols] + r1a[c, at(yi * 8, 8), cols]
+        u_buf[slot_of(l + 1), rows_a, cols] = (u_buf[slot_of(l), rows_a, cols] + val).astype(BF16).astype(F32)
         rdma(5, j, h).start()
-        val = r2b[j, :, cols] + r1b[j, at(xi * 8, 8), cols]
-        u_buf[l + 1, rows_b, cols] = (u_buf[l, rows_b, cols] + val).astype(BF16).astype(F32)
+        val = r2b[c, :, cols] + r1b[c, at(xi * 8, 8), cols]
+        u_buf[slot_of(l + 1), rows_b, cols] = (u_buf[slot_of(l), rows_b, cols] + val).astype(BF16).astype(F32)
         rdma(6, j, h).start()
 
     def ev4(j, h):
@@ -401,9 +428,7 @@
             @pl.loop(0, T // 16)
             def _(i):
                 rows = at(c * T + i * 16, 16, 16)
-                hid_s[rows, halves[h]] = u_buf[n_layers, rows, halves[h]].astype(BF16)
-
-            out_copy(c, h).start()
+                out_ref[0, rows, halves[h]] = u_buf[n_layers % 2, rows, halves[h]].astype(BF16)
 
         if isinstance(j, int):
             if l == n_layers - 1:
@@ -455,8 +480,6 @@
             (ev6, 0, 0)):
         guarded(stage, z - back, h)
 
-    pltpu.make_async_copy(hid_s, out_ref.at[0], o_sem).wait()
-
 
 def solution(mesh):
     tp_size = mesh.shape['tp']
@@ -475,27 +498,36 @@
         conv_w = width + 2 * STATE
         n_chunks = n_tok // T
         n_items = n_layers * n_chunks
-        any_spec = pl.BlockSpec(memory_space=pl.ANY)
+        any_spec = pl.BlockSpec(memory_space=pltpu.HBM)
         vmem_spec = pl.BlockSpec(memory_space=pltpu.VMEM)
         dma = pltpu.SemaphoreType.DMA
         return pl.pallas_call(
             functools.partial(mixer_kernel, n_layers, n_chunks, width * tp_size),
             out_shape=jax.ShapeDtypeStruct(hidden.shape, BF16),
-            in_specs=[any_spec, vmem_spec, any_spec, any_spec, any_spec, any_spec] + [vmem_spec] * 8 + [any_spec],
-            out_specs=any_spec,
+            in_specs=[any_spec] * 15,
+            out_specs=vmem_spec,
             scratch_shapes=[
+                pltpu.VMEM(norm_w.shape, BF16),
+                pltpu.VMEM(conv_x.shape, BF16),
+                pltpu.VMEM(conv_bc.shape, BF16),
+                pltpu.VMEM(bias_x.shape, BF16),
+                pltpu.VMEM(bias_bc.shape, BF16),
+                pltpu.VMEM(dt_bias.shape, F32),
+                pltpu.VMEM(a_log.shape, F32),
+                pltpu.VMEM(d_skip.shape, F32),
+                pltpu.VMEM(gate_w.shape, BF16),
                 pltpu.VMEM((n_layers, d_model, conv_w + 128 + width), BF16),
                 pltpu.VMEM((n_layers, width, d_model), BF16),
                 pltpu.VMEM((n_heads, n_layers, d_model), BF16),
                 pltpu.VMEM((16 * n_layers, d_model), F32),
                 pltpu.VMEM((n_tok, d_model), BF16),
-                pltpu.VMEM((n_layers + 1, n_tok, d_model), F32),
+                pltpu.VMEM((2, n_tok, d_model), F32),
                 pltpu.VMEM((T, d_model), F32),
-                pltpu.VMEM((n_items, T // 2, d_model), F32),
-                pltpu.VMEM((n_items, 16, d_model), F32),
-                pltpu.VMEM((n_items, 16, d_model), F32),
-                pltpu.VMEM((n_items, 8, d_model), F32),
-                pltpu.VMEM((n_items, 8, d_model), F32),
+                pltpu.VMEM((n_chunks, T // 2, d_model), F32),
+                pltpu.VMEM((n_chunks, 16, d_model), F32),
+                pltpu.VMEM((n_chunks, 16, d_model), F32),
+                pltpu.VMEM((n_chunks, 8, d_model), F32),
+                pltpu.VMEM((n_chunks, 8, d_model), F32),
                 pltpu.VMEM((T, d_model), BF16),
                 pltpu.VMEM((T + 8, conv_w), F32),
                 pltpu.VMEM((T, 128 + width), F32),
@@ -521,16 +553,17 @@
                 pltpu.VMEM((n_layers, 1, width), F32),
                 dma((n_layers, 3)),
                 dma((3,)),
-                dma(()),
+                dma((9,)),
                 dma((n_chunks, 2, 6)),
                 dma((n_chunks, 2, 6)),
                 dma((n_chunks,)),
                 dma((n_chunks,)),
             ],
             compiler_params=pltpu.CompilerParams(
-                collective_id=0, has_side_effects=True, vmem_limit_bytes=67043328),
+                collective_id=0, has_side_effects=True, vmem_limit_bytes=50000000),
             name="mixer",
-        )(hidden, norm_w, w_z, w_x, w_bc, jnp.transpose(w_dt, (2, 0, 1)), conv_x, conv_bc, bias_x, bias_bc, dt_bias,
-          a_log, d_skip, gate_w, w_out)
+        )(*[pltpu.with_memory_space_constraint(arg, pltpu.HBM) for arg in (
+            hidden, norm_w, w_z, w_x, w_bc, jnp.transpose(w_dt, (2, 0, 1)), conv_x, conv_bc, bias_x, bias_bc, dt_bias,
+            a_log, d_skip, gate_w, w_out)])
 
     return jax.shard_map(device_forward, mesh=mesh, in_specs=in_specs, out_specs=P('dp'), check_vma=False)

time: 112 us -> 108 us (0.964)
  Pallas kernels: 108 us -> 106 us
  local copies, waits for them, and re-layouts: 3.4 us -> 1.49 us
    pallas_call x1, Pallas kernels: 108 us -> 106 us  [device_forward(): pl.pallas_call(functools.partial(mixer_kernel, n_layers, n_chunks, width...]
    unnamed x1, local copies, waits for them, and re-layouts: 3.4 us -> 1.49 us
where the time goes in v3:
time: 108 us
  Pallas kernels  106 us (98%)
  local copies, waits for them, and re-layouts  1.49 us (1%)
    pallas_call x1, Pallas kernels, device_forward(): pl.pallas_call(functools.partial(mixer_kernel, n_layers, n_chunks, width...  106 us

profile of v3, /device:TPU:0, one launch (start us, length us, event | category | flops | bytes accessed | tf_op | source)
XLA Modules:
  0.0 107.8 jit_solution(9308865925820900141)
XLA Ops:
  0.0 106.3 %mixer.1 = bf16[1,512,2560]{2,1,0:T(8,128)(2,1)S(1)} custom-call(bf16[1,512,2560]{2,1,0:T(8,128)(2,1)} %hid_ref.1, bf16[2,2560]{1,0:T(2,128)(2,1)} %norm_hbm.1, bf16[2,2560,640]{2,1,0:T(8,128)(2,1)} %wz_ref.1, bf16[2,2560,640]{2,1,0:T(8,128)(2,1)} %wx_ref.1, bf16[2,2560,128]{2,1,0:T(8,128)(2,1)} %wbc_ref.1, bf16[10,2,2560]{2,1,0:T(2,128)(2,1)} %bitcast.1, ...), custom_call_target="tpu_custom_call" | custom-call | tf_op jit(solution)/shard_map/mixer/pallas_call | solution.py:504
  106.3 1.5 %copy.17 = bf16[1,512,2560]{2,1,0:T(8,128)(2,1)} copy(bf16[1,512,2560]{2,1,0:T(8,128)(2,1)S(1)} %mixer.1) | data formatting | bytes 5242880

commit v4 on v3

--- a/solution.py
+++ b/solution.py
@@ -14,6 +14,19 @@
 HI = lax.Precision.HIGHEST
 F32 = jnp.float32
 BF16 = jnp.bfloat16
+
+SLOTS = (
+    ((4, 0, 3, 0, (), ()), (3, 1, 2, 0, (1,), ()),),
+    ((2, 1, 2, 0, (2,), ()), (5, 0, 3, 0, (1,), ()), (1, 0, 1, 1, (), (0, 2)), (1, 1, 1, 0, (1,), ()), (1, 1, 1, 0, (), (0, 1, 2)),),
+    ((3, 1, 2, 0, (), (0, 1, 2)), (1, 0, 1, 1, (2,), ()), (3, 0, 2, 0, (0,), ()), (1, 1, 1, 1, (0,), ()),),
+    ((5, 1, 3, 0, (2,), ()),),
+    ((1, 0, 1, 0, (0,), ()), (5, 1, 3, 0, (), (0, 2)), (2, 0, 1, 0, (1,), ()), (6, 1, 3, 0, (), (0, 1)), (5, 0, 3, 0, (2,), ()), (3, 1, 2, 0, (2,), ()), (3, 0, 2, 0, (), (0,)), (5, 1, 3, 0, (0,), ()),),
+    ((6, 0, 3, 0, (1,), ()), (1, 1, 1, 0, (2,), ()), (5, 0, 3, 0, (0,), ()), (2, 0, 1, 0, (), (0, 1)),),
+    ((2, 1, 1, 0, (), (1, 2)), (5, 0, 3, 0, (), (0, 1, 2)), (6, 1, 3, 0, (1,), ()), (4, 1, 2, 0, (), (0, 2)),),
+    ((6, 0, 3, 0, (0,), ()), (6, 0, 3, 0, (), (0, 1, 2)), (2, 1, 1, 0, (1,), ()),),
+    ((2, 0, 1, 0, (0,), ()), (4, 1, 2, 0, (0,), ()), (4, 1, 2, 0, (2,), ()), (6, 1, 3, 0, (0,), ()), (6, 0, 3, 0, (2,), ()), (3, 1, 1, 0, (0,), ()),),
+)
+DRAIN = ((4, 0, 5, 0), (1, 1, 7, 1), (5, 1, 5, 0), (1, 0, 7, 0), (2, 1, 7, 0), (3, 0, 6, 0), (3, 1, 6, 0), (5, 0, 5, 0), (2, 0, 7, 0), (3, 1, 7, 0), (4, 0, 6, 0), (3, 0, 7, 0), (6, 1, 5, 0), (4, 1, 6, 0), (5, 0, 6, 0), (4, 1, 7, 0), (4, 0, 7, 0), (6, 0, 6, 0), (5, 1, 6, 0), (5, 1, 7, 0), (5, 0, 7, 0), (6, 1, 6, 0), (6, 0, 5, 0), (6, 1, 7, 0), (6, 0, 7, 0))
 
 
 def mixer_kernel(n_layers, n_chunks, inner_width,
@@ -90,33 +103,40 @@
         (gate_hbm, gate_ref)))]
 
     hid_copy(0).start()
-    for cp in small:
+    small[0].start()
+    dt_weight_copy().start()
+    for cp in conv_weight_copies(0):
         cp.start()
-    dt_weight_copy().start()
-    start_in_weights(0)
+    for cp in small[1:]:
+        cp.start()
 
     barrier = pltpu.get_barrier_semaphore()
     for rel in relations:
         pl.semaphore_signal(barrier, inc=1, device_id=peer_id(*rel))
 
-    for cp in small:
-        cp.wait()
     lane = lax.broadcasted_iota(jnp.int32, (1, 128), 1)
+    small[0].wait()
+    gate_weight_copy(0).start()
     for l in range(n_layers):
         norm_s[l] = norm_ref[l:l + 1, :].astype(F32)
-        cw_s[l, :, 0:width] = convx_ref[l].astype(F32)
-        cw_s[l, :, width:conv_w] = convbc_ref[l].astype(F32)
-        cb_s[l, :, 0:width] = biasx_ref[l:l + 1, :].astype(F32)
-        cb_s[l, :, width:conv_w] = biasbc_ref[l:l + 1, :].astype(F32)
-        gate_s[l] = gate_ref[l:l + 1, :].astype(F32)
-        dtb_s[l] = jnp.zeros((1, 128), F32)
-        nega_s[l] = jnp.zeros((1, 128), F32)
-        dtb_s[l, :, 0:n_heads] = dtb_ref[l:l + 1, :]
-        nega_s[l, :, 0:n_heads] = -jnp.exp(alog_ref[l:l + 1, :])
-        for p in range(n_pairs):
-            d0 = dskip_ref[l:l + 1, 2 * p:2 * p + 1]
-            d1 = dskip_ref[l:l + 1, 2 * p + 1:2 * p + 2]
-            dsk_s[l, :, 128 * p:128 * (p + 1)] = jnp.where(lane < HEAD, d0, d1)
+
+    def small_parameters():
+        for cp in small[1:]:
+            cp.wait()
+        for l in range(n_layers):
+            cw_s[l, :, 0:width] = convx_ref[l].astype(F32)
+            cw_s[l, :, width:conv_w] = convbc_ref[l].astype(F32)
+            cb_s[l, :, 0:width] = biasx_ref[l:l + 1, :].astype(F32)
+            cb_s[l, :, width:conv_w] = biasbc_ref[l:l + 1, :].astype(F32)
+            gate_s[l] = gate_ref[l:l + 1, :].astype(F32)
+            dtb_s[l] = jnp.zeros((1, 128), F32)
+            nega_s[l] = jnp.zeros((1, 128), F32)
+            dtb_s[l, :, 0:n_heads] = dtb_ref[l:l + 1, :]
+            nega_s[l, :, 0:n_heads] = -jnp.exp(alog_ref[l:l + 1, :])
+            for p in range(n_pairs):
+                d0 = dskip_ref[l:l + 1, 2 * p:2 * p + 1]
+                d1 = dskip_ref[l:l + 1, 2 * p + 1:2 * p + 2]
+                dsk_s[l, :, 128 * p:128 * (p + 1)] = jnp.where(lane < HEAD, d0, d1)
 
     def rdma(kind, j, h):
         l, c = split_item(j)
@@ -226,6 +246,19 @@
     def in_conv(j):
         l, c = split_item(j)
 
+        @pl.when(c == 0)
+        def _():
+            both = w_in.at[l, :, pl.ds(0, conv_w)]
+            pltpu.make_async_copy(both, both, w_sem.at[l, 0]).wait()
+
+        h = h_buf[...]
+        for n in range(0, conv_w, 256):
+            r = jnp.dot(h, w_in[l, :, n:n + 256], preferred_element_type=F32)
+            c_buf[8:8 + T, n:n + 256] = r.astype(BF16).astype(F32)
+
+    def in_gate(j):
+        l, c = split_item(j)
+
         @pl.when(j == 0)
         def _():
             dt_weight_copy().wait()
@@ -240,25 +273,13 @@
         def _():
             w_in[l, :, conv_w:conv_w + 128] = jnp.zeros((d_model, 128), BF16)
             w_in[l, :, conv_w:conv_w + 16] = wdt_f[at(16 * l, 16), :].T.astype(BF16)
-            both = w_in.at[l, :, pl.ds(0, conv_w)]
-            pltpu.make_async_copy(both, both, w_sem.at[l, 0]).wait()
-
-        h = h_buf[...]
-        for n in range(0, conv_w, 256):
-            r = jnp.dot(h, w_in[l, :, n:n + 256], preferred_element_type=F32)
-            c_buf[8:8 + T, n:n + 256] = r.astype(BF16).astype(F32)
-
-    def in_gate(j):
-        l, c = split_item(j)
-
-        @pl.when(c == 0)
-        def _():
             gate_weight_copy(l).wait()
 
         @pl.when(j == 0)
         def _():
             out_weight_copy(0).start()
             hid_copy(1).start()
+            small_parameters()
 
         h = h_buf[...]
         for n in range(0, width + 128, 256):
@@ -367,9 +388,9 @@
             f = rs / jnp.maximum(own, 1e-30)
             f_s[k] = jnp.broadcast_to(f, (T, T)).T
 
-    def ev1(j, h):
+    def ev1(j, h, first):
         _, c = split_item(j)
-        if h == 1:
+        if first:
             factors(j)
         mine = core * (T // 2)
         rdma(0, j, h).wait()
@@ -388,7 +409,7 @@
         add(xi * 16)
         add(32 + yi * 16)
 
-    def ev2(j, h):
+    def ev2(j, h, first):
         _, c = split_item(j)
         cols = halves[h]
         wait_pair(1, j, h)
@@ -397,7 +418,7 @@
         r1b[c, :, cols] += r0[c, at(32 + yi * 16, 16), cols]
         rdma(4, j, h).start()
 
-    def ev3(j, h):
+    def ev3(j, h, first):
         l, c = split_item(j)
         cols = halves[h]
         base = c * T + core * (T // 2)
@@ -411,16 +432,16 @@
         u_buf[slot_of(l + 1), rows_b, cols] = (u_buf[slot_of(l), rows_b, cols] + val).astype(BF16).astype(F32)
         rdma(6, j, h).start()
 
-    def ev4(j, h):
+    def ev4(j, h, first):
         wait_pair(5, j, h)
         rdma(7, j, h).start()
         rdma(8, j, h).start()
 
-    def ev5(j, h):
+    def ev5(j, h, first):
         wait_pair(7, j, h)
         rdma(9, j, h).start()
 
-    def ev6(j, h):
+    def ev6(j, h, first):
         l, c = split_item(j)
         rdma(9, j, h).wait()
 
@@ -436,49 +457,44 @@
         else:
             pl.when(l == n_layers - 1)(finish)
 
-    def guarded(stage, j, *args):
-        def run():
-            with jax.named_scope(stage.__name__ + "".join(str(a) for a in args)):
-                stage(j, *args)
-
-        if isinstance(j, int):
-            if 0 <= j < n_items:
-                run()
-        else:
-            pl.when(jnp.logical_and(j >= 0, j < n_items))(run)
+    steps = {1: ev1, 2: ev2, 3: ev3, 4: ev4, 5: ev5, 6: ev6}
+
+    def run_step(step, item, h, first):
+        with jax.named_scope("ev%d%d" % (step, h)):
+            steps[step](item, h, first)
+
+    def slot(k, j):
+        for step, h, delta, first, only, skip in SLOTS[k]:
+            if only:
+                for item in only:
+                    pl.when(j == item + delta)(functools.partial(run_step, step, item, h, first))
+            else:
+                item = j - delta
+                there = jnp.logical_and(item >= 0, item < n_items)
+                for other in skip:
+                    there = jnp.logical_and(there, item != other)
+                pl.when(there)(functools.partial(run_step, step, item, h, first))
 
     pl.semaphore_wait(barrier, len(relations))
+
+    pieces = (in_norm, in_conv, in_gate, scan_prep, scan_a, scan_b, functools.partial(out_proj, h=0),
+              functools.partial(out_proj, h=1))
+    names = ("norm", "conv", "gate", "prep", "scan_a", "scan_b", "out0", "out1")
 
     @pl.loop(0, n_items)
     def _(j):
-        guarded(ev6, j - 4, 0)
-        guarded(in_norm, j)
-        guarded(ev3, j - 2, 1)
-        guarded(ev1, j - 1, 1)
-        guarded(ev3, j - 2, 0)
-        guarded(in_conv, j)
-        guarded(ev5, j - 3, 1)
-        guarded(ev1, j - 1, 0)
-        guarded(in_gate, j)
-        guarded(ev4, j - 2, 1)
-        guarded(scan_prep, j)
-        guarded(ev5, j - 3, 0)
-        guarded(scan_a, j)
-        guarded(ev2, j - 1, 1)
-        guarded(scan_b, j)
-        guarded(out_proj, j, 0)
-        guarded(ev6, j - 3, 1)
-        guarded(ev4, j - 2, 0)
-        guarded(out_proj, j, 1)
-        guarded(ev2, j - 1, 0)
-
-    z = n_items - 1
-    for stage, back, h in (
-            (ev6, 3, 0), (ev5, 2, 1), (ev3, 1, 1), (ev6, 2, 1), (ev1, 0, 1), (ev1, 0, 0), (ev5, 2, 0), (ev3, 1, 0),
-            (ev6, 2, 0), (ev4, 1, 1), (ev2, 0, 1), (ev2, 0, 0), (ev4, 1, 0), (ev5, 1, 1), (ev3, 0, 1), (ev6, 1, 1),
-            (ev3, 0, 0), (ev5, 1, 0), (ev4, 0, 1), (ev6, 1, 0), (ev4, 0, 0), (ev5, 0, 1), (ev6, 0, 1), (ev5, 0, 0),
-            (ev6, 0, 0)):
-        guarded(stage, z - back, h)
+        for k, (piece, name) in enumerate(zip(pieces, names)):
+            slot(k, j)
+
+            @pl.when(jnp.logical_and(j >= 0, j < n_items))
+            def _():
+                with jax.named_scope(name):
+                    piece(j)
+
+        slot(len(pieces), j)
+
+    for step, h, item, first in DRAIN:
+        run_step(step, item, h, first)
 
 
 def solution(mesh):

time: 108 us -> 106 us (0.981)
  Pallas kernels: 106 us -> 104 us
    pallas_call x1, Pallas kernels: 106 us -> 104 us  [device_forward(): pl.pallas_call(functools.partial(mixer_kernel, n_layers, n_chunks, width...]
where the time goes in v4:
time: 106 us
  Pallas kernels  104 us (98%)
  local copies, waits for them, and re-layouts  1.49 us (1%)
    pallas_call x1, Pallas kernels, device_forward(): pl.pallas_call(functools.partial(mixer_kernel, n_layers, n_chunks, width...  104 us

profile of v4, /device:TPU:0, one launch (start us, length us, event | category | flops | bytes accessed | tf_op | source)
XLA Modules:
  0.0 105.9 jit_solution(8872858290292349076)
XLA Ops:
  0.0 104.3 %mixer.1 = bf16[1,512,2560]{2,1,0:T(8,128)(2,1)S(1)} custom-call(bf16[1,512,2560]{2,1,0:T(8,128)(2,1)} %hid_ref.1, bf16[2,2560]{1,0:T(2,128)(2,1)} %norm_hbm.1, bf16[2,2560,640]{2,1,0:T(8,128)(2,1)} %wz_ref.1, bf16[2,2560,640]{2,1,0:T(8,128)(2,1)} %wx_ref.1, bf16[2,2560,128]{2,1,0:T(8,128)(2,1)} %wbc_ref.1, bf16[10,2,2560]{2,1,0:T(2,128)(2,1)} %bitcast.1, ...), custom_call_target="tpu_custom_call" | custom-call | tf_op jit(solution)/shard_map/mixer/pallas_call | solution.py:520
  104.4 1.5 %copy.17 = bf16[1,512,2560]{2,1,0:T(8,128)(2,1)} copy(bf16[1,512,2560]{2,1,0:T(8,128)(2,1)S(1)} %mixer.1) | data formatting | bytes 5242880

commit v5 on v4

--- a/solution.py
+++ b/solution.py
@@ -16,13 +16,13 @@
 BF16 = jnp.bfloat16
 
 SLOTS = (
-    ((4, 0, 3, 0, (), ()), (3, 1, 2, 0, (1,), ()),),
-    ((2, 1, 2, 0, (2,), ()), (5, 0, 3, 0, (1,), ()), (1, 0, 1, 1, (), (0, 2)), (1, 1, 1, 0, (1,), ()), (1, 1, 1, 0, (), (0, 1, 2)),),
+    ((4, 0, 3, 0, (), ()), (3, 1, 2, 0, (1,), ()), (1, 1, 1, 1, (1,), ()),),
+    ((2, 1, 2, 0, (2,), ()), (1, 0, 1, 1, (), (0, 1, 2)), (1, 0, 1, 0, (), (0, 2, 3, 4, 5, 6)), (5, 0, 3, 0, (1,), ()), (1, 1, 1, 0, (), (0, 1, 2)),),
     ((3, 1, 2, 0, (), (0, 1, 2)), (1, 0, 1, 1, (2,), ()), (3, 0, 2, 0, (0,), ()), (1, 1, 1, 1, (0,), ()),),
     ((5, 1, 3, 0, (2,), ()),),
-    ((1, 0, 1, 0, (0,), ()), (5, 1, 3, 0, (), (0, 2)), (2, 0, 1, 0, (1,), ()), (6, 1, 3, 0, (), (0, 1)), (5, 0, 3, 0, (2,), ()), (3, 1, 2, 0, (2,), ()), (3, 0, 2, 0, (), (0,)), (5, 1, 3, 0, (0,), ()),),
+    ((1, 0, 1, 0, (0,), ()), (5, 1, 3, 0, (), (0, 2)), (6, 1, 3, 0, (), (0, 1)), (5, 0, 3, 0, (2,), ()), (3, 1, 2, 0, (2,), ()), (3, 0, 2, 0, (), (0,)), (5, 1, 3, 0, (0,), ()),),
     ((6, 0, 3, 0, (1,), ()), (1, 1, 1, 0, (2,), ()), (5, 0, 3, 0, (0,), ()), (2, 0, 1, 0, (), (0, 1)),),
-    ((2, 1, 1, 0, (), (1, 2)), (5, 0, 3, 0, (), (0, 1, 2)), (6, 1, 3, 0, (1,), ()), (4, 1, 2, 0, (), (0, 2)),),
+    ((2, 1, 1, 0, (), (1, 2)), (5, 0, 3, 0, (), (0, 1, 2)), (6, 1, 3, 0, (1,), ()), (4, 1, 2, 0, (), (0, 2)), (2, 0, 1, 0, (1,), ()),),
     ((6, 0, 3, 0, (0,), ()), (6, 0, 3, 0, (), (0, 1, 2)), (2, 1, 1, 0, (1,), ()),),
     ((2, 0, 1, 0, (0,), ()), (4, 1, 2, 0, (0,), ()), (4, 1, 2, 0, (2,), ()), (6, 1, 3, 0, (0,), ()), (6, 0, 3, 0, (2,), ()), (3, 1, 1, 0, (0,), ()),),
 )
@@ -102,8 +102,8 @@
         (biasbc_hbm, biasbc_ref), (dtb_hbm, dtb_ref), (alog_hbm, alog_ref), (dskip_hbm, dskip_ref),
         (gate_hbm, gate_ref)))]
 
+    small[0].start()
     hid_copy(0).start()
-    small[0].start()
     dt_weight_copy().start()
     for cp in conv_weight_copies(0):
         cp.start()
@@ -246,21 +246,9 @@
     def in_conv(j):
         l, c = split_item(j)
 
-        @pl.when(c == 0)
-        def _():
-            both = w_in.at[l, :, pl.ds(0, conv_w)]
-            pltpu.make_async_copy(both, both, w_sem.at[l, 0]).wait()
-
-        h = h_buf[...]
-        for n in range(0, conv_w, 256):
-            r = jnp.dot(h, w_in[l, :, n:n + 256], preferred_element_type=F32)
-            c_buf[8:8 + T, n:n + 256] = r.astype(BF16).astype(F32)
-
-    def in_gate(j):
-        l, c = split_item(j)
-
         @pl.when(j == 0)
         def _():
+            small_parameters()
             dt_weight_copy().wait()
             for k in range(n_layers):
                 wdt_f[16 * k + 8:16 * k + 16, :] = jnp.zeros((8, d_model), F32)
@@ -271,6 +259,19 @@
 
         @pl.when(c == 0)
         def _():
+            both = w_in.at[l, :, pl.ds(0, conv_w)]
+            pltpu.make_async_copy(both, both, w_sem.at[l, 0]).wait()
+
+        h = h_buf[...]
+        for n in range(0, conv_w, 256):
+            r = jnp.dot(h, w_in[l, :, n:n + 256], preferred_element_type=F32)
+            c_buf[8:8 + T, n:n + 256] = r.astype(BF16).astype(F32)
+
+    def in_gate(j):
+        l, c = split_item(j)
+
+        @pl.when(c == 0)
+        def _():
             w_in[l, :, conv_w:conv_w + 128] = jnp.zeros((d_model, 128), BF16)
             w_in[l, :, conv_w:conv_w + 16] = wdt_f[at(16 * l, 16), :].T.astype(BF16)
             gate_weight_copy(l).wait()
@@ -279,7 +280,6 @@
         def _():
             out_weight_copy(0).start()
             hid_copy(1).start()
-            small_parameters()
 
         h = h_buf[...]
         for n in range(0, width + 128, 256):

time: 106 us -> 105 us (level)
    pallas_call x1, Pallas kernels: 104 us -> 103 us  [device_forward(): pl.pallas_call(functools.partial(mixer_kernel, n_layers, n_chunks, width...]
where the time goes in v5:
time: 105 us
  Pallas kernels  103 us (98%)
  local copies, waits for them, and re-layouts  1.49 us (1%)
    pallas_call x1, Pallas kernels, device_forward(): pl.pallas_call(functools.partial(mixer_kernel, n_layers, n_chunks, width...  103 us

profile of v5, /device:TPU:0, one launch (start us, length us, event | category | flops | bytes accessed | tf_op | source)
XLA Modules:
  0.0 104.7 jit_solution(6654478545834416159)
XLA Ops:
  0.0 103.2 %mixer.1 = bf16[1,512,2560]{2,1,0:T(8,128)(2,1)S(1)} custom-call(bf16[1,512,2560]{2,1,0:T(8,128)(2,1)} %hid_ref.1, bf16[2,2560]{1,0:T(2,128)(2,1)} %norm_hbm.1, bf16[2,2560,640]{2,1,0:T(8,128)(2,1)} %wz_ref.1, bf16[2,2560,640]{2,1,0:T(8,128)(2,1)} %wx_ref.1, bf16[2,2560,128]{2,1,0:T(8,128)(2,1)} %wbc_ref.1, bf16[10,2,2560]{2,1,0:T(2,128)(2,1)} %bitcast.1, ...), custom_call_target="tpu_custom_call" | custom-call | tf_op jit(solution)/shard_map/mixer/pallas_call | solution.py:520
  103.2 1.5 %copy.17 = bf16[1,512,2560]{2,1,0:T(8,128)(2,1)} copy(bf16[1,512,2560]{2,1,0:T(8,128)(2,1)S(1)} %mixer.1) | data formatting | bytes 5242880

commit v6 on v5

--- a/solution.py
+++ b/solution.py
@@ -16,17 +16,17 @@
 BF16 = jnp.bfloat16
 
 SLOTS = (
-    ((4, 0, 3, 0, (), ()), (3, 1, 2, 0, (1,), ()), (1, 1, 1, 1, (1,), ()),),
-    ((2, 1, 2, 0, (2,), ()), (1, 0, 1, 1, (), (0, 1, 2)), (1, 0, 1, 0, (), (0, 2, 3, 4, 5, 6)), (5, 0, 3, 0, (1,), ()), (1, 1, 1, 0, (), (0, 1, 2)),),
-    ((3, 1, 2, 0, (), (0, 1, 2)), (1, 0, 1, 1, (2,), ()), (3, 0, 2, 0, (0,), ()), (1, 1, 1, 1, (0,), ()),),
-    ((5, 1, 3, 0, (2,), ()),),
-    ((1, 0, 1, 0, (0,), ()), (5, 1, 3, 0, (), (0, 2)), (6, 1, 3, 0, (), (0, 1)), (5, 0, 3, 0, (2,), ()), (3, 1, 2, 0, (2,), ()), (3, 0, 2, 0, (), (0,)), (5, 1, 3, 0, (0,), ()),),
-    ((6, 0, 3, 0, (1,), ()), (1, 1, 1, 0, (2,), ()), (5, 0, 3, 0, (0,), ()), (2, 0, 1, 0, (), (0, 1)),),
-    ((2, 1, 1, 0, (), (1, 2)), (5, 0, 3, 0, (), (0, 1, 2)), (6, 1, 3, 0, (1,), ()), (4, 1, 2, 0, (), (0, 2)), (2, 0, 1, 0, (1,), ()),),
-    ((6, 0, 3, 0, (0,), ()), (6, 0, 3, 0, (), (0, 1, 2)), (2, 1, 1, 0, (1,), ()),),
-    ((2, 0, 1, 0, (0,), ()), (4, 1, 2, 0, (0,), ()), (4, 1, 2, 0, (2,), ()), (6, 1, 3, 0, (0,), ()), (6, 0, 3, 0, (2,), ()), (3, 1, 1, 0, (0,), ()),),
+    ((1, 0, 1, 1, (), (0, 1, 2)), (1, 1, 1, 0, (2,), ()),),
+    ((1, 0, 1, 1, (0,), ()), (1, 0, 1, 1, (1,), ()),),
+    ((5, 1, 3, 0, (0,), ()), (5, 0, 3, 0, (2,), ()), (3, 1, 2, 0, (2,), ()), (1, 1, 1, 0, (), (0, 1, 2)), (5, 0, 3, 0, (), (0, 1, 2)),),
+    ((3, 0, 2, 0, (1,), ()), (3, 0, 2, 0, (0,), ()), (5, 1, 3, 0, (2,), ()), (5, 0, 3, 0, (0,), ()), (1, 1, 1, 0, (0,), ()), (3, 1, 2, 0, (1,), ()),),
+    ((3, 1, 2, 0, (), (1, 2)), (5, 1, 3, 0, (), (0, 1, 2)), (1, 1, 1, 0, (1,), ()), (5, 0, 3, 0, (1,), ()), (2, 0, 1, 1, (), (0,)),),
+    ((6, 0, 3, 0, (), (0, 2)), (2, 1, 1, 0, (2,), ()), (4, 1, 2, 0, (2,), ()), (4, 0, 2, 0, (), (1,)),),
+    ((4, 1, 2, 0, (1,), ()), (6, 0, 3, 0, (2,), ()), (6, 1, 3, 0, (), (0, 1, 2)), (2, 0, 1, 1, (0,), ()), (5, 1, 3, 0, (1,), ()),),
+    ((4, 0, 2, 0, (1,), ()), (2, 1, 1, 0, (1,), ()), (6, 0, 3, 0, (0,), ()), (2, 1, 1, 0, (), (1, 2)), (6, 1, 3, 0, (0,), ()), (4, 1, 2, 0, (), (0, 1, 2)), (3, 0, 1, 0, (), (0, 1, 2)), (4, 1, 2, 0, (0,), ()),),
+    ((6, 1, 3, 0, (2,), ()), (6, 1, 3, 0, (1,), ()), (1, 0, 0, 1, (2,), ()), (3, 0, 1, 0, (2,), ()),),
 )
-DRAIN = ((4, 0, 5, 0), (1, 1, 7, 1), (5, 1, 5, 0), (1, 0, 7, 0), (2, 1, 7, 0), (3, 0, 6, 0), (3, 1, 6, 0), (5, 0, 5, 0), (2, 0, 7, 0), (3, 1, 7, 0), (4, 0, 6, 0), (3, 0, 7, 0), (6, 1, 5, 0), (4, 1, 6, 0), (5, 0, 6, 0), (4, 1, 7, 0), (4, 0, 7, 0), (6, 0, 6, 0), (5, 1, 6, 0), (5, 1, 7, 0), (5, 0, 7, 0), (6, 1, 6, 0), (6, 0, 5, 0), (6, 1, 7, 0), (6, 0, 7, 0))
+DRAIN = ((1, 1, 7, 1), (5, 1, 5, 0), (1, 0, 7, 0), (2, 1, 7, 1), (3, 1, 6, 0), (5, 0, 5, 0), (2, 0, 7, 0), (3, 1, 7, 0), (4, 0, 6, 0), (3, 0, 7, 0), (6, 1, 5, 0), (4, 1, 6, 0), (5, 0, 6, 0), (4, 1, 7, 0), (4, 0, 7, 0), (6, 0, 6, 0), (5, 1, 6, 0), (5, 1, 7, 0), (5, 0, 7, 0), (6, 1, 6, 0), (6, 0, 5, 0), (6, 1, 7, 0), (6, 0, 7, 0))
 
 
 def mixer_kernel(n_layers, n_chunks, inner_width,
@@ -180,14 +180,14 @@
         _, c = split_item(j)
         return pltpu.make_async_remote_copy(
             src_ref=stats.at[j, pl.ds(0, 1), :], dst_ref=stats.at[j, pl.ds(r + 1, 1), :],
-            send_sem=st_send.at[c], recv_sem=st_recv.at[c],
+            send_sem=st_send.at[c, min(r, 1)], recv_sem=st_recv.at[c, min(r, 1)],
             device_id=peer_id(*relations[r]), device_id_type=pl.DeviceIdType.MESH)
 
-    def wait_stats(j):
+    def wait_stats(j, k):
         _, c = split_item(j)
-        rows = stats.at[j, pl.ds(1, len(relations)), :]
-        pltpu.make_async_copy(rows, rows, st_send.at[c]).wait()
-        pltpu.make_async_copy(rows, rows, st_recv.at[c]).wait()
+        rows = stats.at[j, pl.ds(1, 1) if k == 0 else pl.ds(2, len(relations) - 1), :]
+        pltpu.make_async_copy(rows, rows, st_send.at[c, k]).wait()
+        pltpu.make_async_copy(rows, rows, st_recv.at[c, k]).wait()
 
     def in_norm(j):
         l, c = split_item(j)
@@ -379,19 +379,27 @@
             p_buf[:, n:n + 256] = jnp.dot(g, w_o[l, :, n:n + 256], preferred_element_type=F32)
         rdma(0, j, h).start()
 
-    def factors(j):
-        wait_stats(j)
+    def store_factor(k, wanted, held):
+        f_s[k] = jnp.broadcast_to(wanted / jnp.maximum(held, 1e-30), (T, T)).T
+
+    def chip_factors(j):
+        wait_stats(j, 0)
+        st = stats[j, 0:2, :]
+        chip = lax.rsqrt((st[0:1, :] + st[1:2, :]) * (0.5 / width) + EPS)
+        for k in range(2):
+            store_factor(k, chip, lax.rsqrt(st[k:k + 1, :] * (1.0 / width) + EPS))
+
+    def total_factors(j):
+        wait_stats(j, 1)
         st = stats[j]
         rs = lax.rsqrt(jnp.sum(st, axis=0, keepdims=True) * (1.0 / inner_width) + EPS)
-        for k in range(2):
-            own = lax.rsqrt(st[k:k + 1, :] * (1.0 / width) + EPS)
-            f = rs / jnp.maximum(own, 1e-30)
-            f_s[k] = jnp.broadcast_to(f, (T, T)).T
+        for k, row in ((2, 0), (3, 4), (4, 2)):
+            store_factor(k, rs, lax.rsqrt((st[row:row + 1, :] + st[row + 1:row + 2, :]) * (0.5 / width) + EPS))
 
     def ev1(j, h, first):
         _, c = split_item(j)
         if first:
-            factors(j)
+            chip_factors(j)
         mine = core * (T // 2)
         rdma(0, j, h).wait()
 
@@ -411,11 +419,21 @@
 
     def ev2(j, h, first):
         _, c = split_item(j)
-        cols = halves[h]
+        mine = core * (T // 2)
+        if first:
+            total_factors(j)
         wait_pair(1, j, h)
-        r1a[c, :, cols] += r0[c, at(xi * 16, 16), cols]
+
+        def combine(ref, k, off):
+            f_own = f_s[2, at(mine + off, 16), :]
+            f_other = f_s[k, at(mine + off, 16), :]
+            for n in range(h * half, (h + 1) * half, 128):
+                cols = slice(n, n + 128)
+                ref[c, :, cols] = ref[c, :, cols] * f_other + r0[c, at(off, 16), cols] * f_own
+
+        combine(r1a, 3, xi * 16)
         rdma(3, j, h).start()
-        r1b[c, :, cols] += r0[c, at(32 + yi * 16, 16), cols]
+        combine(r1b, 4, 32 + yi * 16)
         rdma(4, j, h).start()
 
     def ev3(j, h, first):
@@ -558,7 +576,7 @@
                 pltpu.VMEM((T, T), F32),
                 pltpu.VMEM((STATE, T), F32),
                 pltpu.VMEM((T, 128), F32),
-                pltpu.VMEM((2, T, T), F32),
+                pltpu.VMEM((5, T, T), F32),
                 pltpu.VMEM((n_items, 8, T), F32),
                 pltpu.VMEM((n_layers, 1, d_model), F32),
                 pltpu.VMEM((n_layers, 4, conv_w), F32),
@@ -572,8 +590,8 @@
                 dma((9,)),
                 dma((n_chunks, 2, 6)),
                 dma((n_chunks, 2, 6)),
-                dma((n_chunks,)),
-                dma((n_chunks,)),
+                dma((n_chunks, 2)),
+                dma((n_chunks, 2)),
             ],
             compiler_params=pltpu.CompilerParams(
                 collective_id=0, has_side_effects=True, vmem_limit_bytes=50000000),

time: 105 us -> 104 us (level)
  no operation moved by 1% of the time
where the time goes in v6:
time: 104 us
  Pallas kernels  103 us (99%)
  local copies, waits for them, and re-layouts  1.49 us (1%)
    pallas_call x1, Pallas kernels, device_forward(): pl.pallas_call(functools.partial(mixer_kernel, n_layers, n_chunks, width...  103 us

profile of v6, /device:TPU:0, one launch (start us, length us, event | category | flops | bytes accessed | tf_op | source)
XLA Modules:
  0.0 104.3 jit_solution(16787503068621458295)
XLA Ops:
  0.0 102.8 %mixer.1 = bf16[1,512,2560]{2,1,0:T(8,128)(2,1)S(1)} custom-call(bf16[1,512,2560]{2,1,0:T(8,128)(2,1)} %hid_ref.1, bf16[2,2560]{1,0:T(2,128)(2,1)} %norm_hbm.1, bf16[2,2560,640]{2,1,0:T(8,128)(2,1)} %wz_ref.1, bf16[2,2560,640]{2,1,0:T(8,128)(2,1)} %wx_ref.1, bf16[2,2560,128]{2,1,0:T(8,128)(2,1)} %wbc_ref.1, bf16[10,2,2560]{2,1,0:T(2,128)(2,1)} %bitcast.1, ...), custom_call_target="tpu_custom_call" | custom-call | tf_op jit(solution)/shard_map/mixer/pallas_call | solution.py:538
  102.8 1.5 %copy.17 = bf16[1,512,2560]{2,1,0:T(8,128)(2,1)} copy(bf16[1,512,2560]{2,1,0:T(8,128)(2,1)S(1)} %mixer.1) | data formatting | bytes 5242880
